TPU v7x, 8 devices: a whole 2x2x1 slice. The times are simulated.
8 devices in a mesh: dp: 1 (over z), ep: 8 (over y, x, core).
Axes of the slice: x: 2, y: 2, z: 1, core: 2. Of those that a mesh axis runs over, the one named last changes fastest.
Arguments:
- hidden: bfloat16 [512, 768], P(('dp', 'ep'))
- self_pos: int32 [512], P(('dp', 'ep'))
- src_len: int32 [512], P(('dp', 'ep'))
- cache_a: bfloat16 [2, 512, 16, 12, 64], P(None, ('dp', 'ep'))
- cross_a: bfloat16 [2, 512, 64, 12, 64], P(None, ('dp', 'ep'))
- cache_b: bfloat16 [2, 512, 16, 12, 64], P(None, ('dp', 'ep'))
- cross_b: bfloat16 [2, 512, 64, 12, 64], P(None, ('dp', 'ep'))
- route_ids: int32 [512, 2], P(('dp', 'ep'))
- ln_gain: float32 [2, 3, 768], replicated
- ln_shift: float32 [2, 3, 768], replicated
- attn_w: bfloat16 [2, 6, 768, 768], replicated
- attn_b: bfloat16 [2, 6, 768], replicated
- ffn_w1: bfloat16 [768, 3072], replicated
- ffn_b1: bfloat16 [3072], replicated
- ffn_w2: bfloat16 [3072, 768], replicated
- ffn_b2: bfloat16 [768], replicated
- router_w: bfloat16 [768, 128], replicated
- exp_w1: bfloat16 [128, 768, 3072], P('ep')
- exp_b1: bfloat16 [128, 3072], P('ep')
- exp_w2: bfloat16 [128, 3072, 768], P('ep')
- exp_b2: bfloat16 [128, 768], P('ep')
Outputs:
- output 1: bfloat16 [512, 768], P(('dp', 'ep'))
- output 2: bfloat16 [2, 512, 16, 12, 64], P(None, ('dp', 'ep'))
- output 3: bfloat16 [2, 512, 16, 12, 64], P(None, ('dp', 'ep'))
All inputs are finite; a program needn't handle non-finite values.
Results may differ from a plain program's by a relative error of at most 0.00603.
Values are sent between devices in bfloat16 or wider.
A program may use at most 1 GiB of HBM per device.

v0:
```python
import functools

import jax
import jax.numpy as jnp
from jax import lax
from jax.experimental import pallas as pl
from jax.experimental.pallas import tpu as pltpu
from jax.sharding import PartitionSpec as P

LN_EPS = 1e-5
F32 = jnp.float32
BF16 = jnp.bfloat16
VMEM = pltpu.VMEM


GROUP = 4
SELF_GROUP = 8
HEAD_PAD = 16


def norm_rows(x_val, gain_vec, shift_vec):
    mean_val = jnp.mean(x_val, axis=-1, keepdims=True)
    centered = x_val - mean_val
    var_val = jnp.mean(centered * centered, axis=-1, keepdims=True)
    return (centered * lax.rsqrt(var_val + LN_EPS) * gain_vec + shift_vec).astype(BF16)


def dense_kernel(pos_sm, len_sm, hid_ref, gain_ref, shift_ref, ab_ref, fb1_ref, fb2_ref,
                 cache_a, cross_a, cache_b, cross_b, aw_hbm, w1_hbm, w2_hbm,
                 hid_out, z_out, cache_a_out, cache_b_out,
                 w_buf, f1_buf, f2_buf, self_buf, cross_buf, q_s, k_s, v_s, ctx_s, cat_s, self_mask, cross_mask,
                 w_sem, f_sem, in_sem, out_sem, cross_sem):
    tok, d_model = hid_ref.shape
    n_heads, self_len, head_dim = self_buf.shape[2:]
    src = cross_buf.shape[3]
    ff = f1_buf.shape[1]
    scale = head_dim ** -0.5
    n_self = tok // SELF_GROUP

    def weight_copy(i):
        return pltpu.make_async_copy(aw_hbm.at[i // 6, i % 6], w_buf.at[i], w_sem.at[i])

    def ffn_copies():
        return (pltpu.make_async_copy(w1_hbm, f1_buf, f_sem.at[0]), pltpu.make_async_copy(w2_hbm, f2_buf, f_sem.at[1]))

    def self_in(cache, g):
        rows = pl.ds(g * SELF_GROUP, SELF_GROUP)
        return pltpu.make_async_copy(cache.at[:, rows], self_buf.at[:, rows], in_sem.at[g])

    def self_out(cache_out, g):
        rows = pl.ds(g * SELF_GROUP, SELF_GROUP)
        return pltpu.make_async_copy(self_buf.at[:, rows], cache_out.at[:, rows], out_sem.at[g])

    def cross_rows(b):
        return pl.multiple_of(((len_sm[b] + 15) // 16) * 16, 16)

    def cross_copy(cross, b):
        rows = pl.ds(0, cross_rows(b))
        return pltpu.make_async_copy(cross.at[:, b, :, rows, :], cross_buf.at[b, :, :, rows, :], cross_sem.at[b])

    for i in range(3):
        weight_copy(i).start()
    for g in range(n_self):
        self_in(cache_a, g).start()
    weight_copy(3).start()
    weight_copy(4).start()

    def first_cross(b, c):
        cross_copy(cross_a, b).start()
        return c
    lax.fori_loop(0, tok, first_cross, 0)
    weight_copy(5).start()
    for cp in ffn_copies():
        cp.start()
    for i in range(6, 12):
        weight_copy(i).start()

    def zero_tail(b, c):
        for part in range(1, src // 16):
            @pl.when(part * 16 >= cross_rows(b))
            def _():
                cross_buf[b, 1, :, part * 16:(part + 1) * 16, :] = jnp.zeros((n_heads, 16, head_dim), BF16)
        return c
    lax.fori_loop(0, tok, zero_tail, 0)

    def build_mask(ref, length):
        row = lax.broadcasted_iota(jnp.int32, ref.shape, 0)
        lane = lax.broadcasted_iota(jnp.int32, ref.shape, 1)
        ref[...] = jnp.where(lane // length == row, lane % length, 1 << 20)
    build_mask(self_mask, self_len)
    build_mask(cross_mask, src)

    def to_heads(ref, val):
        val = val.astype(BF16).astype(F32)
        for h in range(n_heads):
            ref[pl.ds(h, tok, stride=HEAD_PAD), :] = val[:, h * head_dim:(h + 1) * head_dim]

    def from_heads(ref):
        for h in range(0, n_heads, 2):
            two = [ref[pl.ds(h + k, tok, stride=HEAD_PAD), :] for k in range(2)]
            cat_s[:, h * head_dim:(h + 2) * head_dim] = jnp.concatenate(two, axis=1).astype(BF16)
        return cat_s[...]

    def softmax_rows(scores, mask_ref, limit):
        scores = jnp.where(mask_ref[...] < limit, scores * scale, -1e30)
        top = jnp.max(scores, axis=-1, keepdims=True)
        ex = jnp.exp(scores - top)
        return (ex * (1.0 / jnp.sum(ex, axis=-1, keepdims=True))).astype(BF16)

    def attend(q, keys, vals, mask_ref, limit):
        scores = lax.dot_general(q, keys, (((1,), (1,)), ((), ())), preferred_element_type=F32)
        probs = softmax_rows(scores, mask_ref, limit)
        return jnp.dot(probs, vals, preferred_element_type=F32)

    def proj(layer, i, x_bf):
        weight_copy(layer * 6 + i).wait()
        bias = ab_ref[layer, i:i + 1, :].astype(F32)
        return jnp.dot(x_bf, w_buf[layer * 6 + i], preferred_element_type=F32) + bias

    def self_layer(layer, h, cache, cache_out):
        x = norm_rows(h, gain_ref[0, layer:layer + 1, :], shift_ref[0, layer:layer + 1, :])
        to_heads(q_s, proj(layer, 0, x))
        to_heads(k_s, proj(layer, 1, x))
        to_heads(v_s, proj(layer, 2, x))
        row_i = lax.broadcasted_iota(jnp.int32, (self_len, head_dim), 0)

        def body(g, c):
            self_in(cache, g).wait()
            for u in range(SELF_GROUP):
                b = g * SELF_GROUP + u
                hit = row_i == pos_sm[b]
                kv = []
                for which, new in ((0, k_s), (1, v_s)):
                    tiles = []
                    for hd in range(n_heads):
                        row = new[pl.ds(b * HEAD_PAD + hd, self_len, stride=0), :]
                        tile = jnp.where(hit, row, self_buf[which, b, hd].astype(F32)).astype(BF16)
                        self_buf[which, b, hd] = tile
                        tiles.append(tile)
                    kv.append(jnp.concatenate(tiles, axis=0))
                q = q_s[pl.ds(pl.multiple_of(b * HEAD_PAD, HEAD_PAD), HEAD_PAD), :].astype(BF16)
                ctx_s[pl.ds(pl.multiple_of(b * HEAD_PAD, HEAD_PAD), HEAD_PAD), :] = attend(q, kv[0], kv[1], self_mask, pos_sm[b] + 1)
            self_out(cache_out, g).start()
            return c
        lax.fori_loop(0, n_self, body, 0)
        ctx = from_heads(ctx_s)
        return h + proj(layer, 3, ctx)

    def cross_layer(layer, h, cross, after):
        x = norm_rows(h, gain_ref[1, layer:layer + 1, :], shift_ref[1, layer:layer + 1, :])
        to_heads(q_s, proj(layer, 4, x))

        def body(g, c):
            for u in range(GROUP):
                cross_copy(cross, g * GROUP + u).wait()
            for u in range(GROUP):
                b = g * GROUP + u
                rows = pl.ds(pl.multiple_of(b * HEAD_PAD, HEAD_PAD), HEAD_PAD)
                q = q_s[rows, :].astype(BF16)
                keys = cross_buf[b, 0].reshape(n_heads * src, head_dim)
                vals = cross_buf[b, 1].reshape(n_heads * src, head_dim)
                ctx_s[rows, :] = attend(q, keys, vals, cross_mask, len_sm[b])
            if after is not None:
                for u in range(GROUP):
                    cross_copy(after, g * GROUP + u).start()
            return c
        lax.fori_loop(0, tok // GROUP, body, 0)
        ctx = from_heads(ctx_s)
        return h + proj(layer, 5, ctx)

    q_s[...] = jnp.zeros_like(q_s)
    h = hid_ref[...].astype(F32)
    h = self_layer(0, h, cache_a, cache_a_out)
    for g in range(n_self):
        self_out(cache_a_out, g).wait()
        self_in(cache_b, g).start()
    h = cross_layer(0, h, cross_a, cross_b)
    x = norm_rows(h, gain_ref[2, 0:1, :], shift_ref[2, 0:1, :])
    for cp in ffn_copies():
        cp.wait()
    acc = h + fb2_ref[...].astype(F32)
    for f in range(0, ff, d_model):
        inner = jnp.dot(x, f1_buf[:, f:f + d_model], preferred_element_type=F32) + fb1_ref[:, f:f + d_model].astype(F32)
        inner = jnp.maximum(inner, 0.0).astype(BF16)
        acc = acc + jnp.dot(inner, f2_buf[f:f + d_model, :], preferred_element_type=F32)
    h = acc
    h = self_layer(1, h, cache_b, cache_b_out)
    h = cross_layer(1, h, cross_b, None)
    hid_out[...] = h
    z_out[...] = norm_rows(h, gain_ref[2, 1:2, :], shift_ref[2, 1:2, :])
    for g in range(n_self):
        self_out(cache_b_out, g).wait()


def dense_layers(hidden, self_pos, src_len, cache_a, cross_a, cache_b, cross_b, ln_gain, ln_shift, attn_w, attn_b, ffn_w1, ffn_b1, ffn_w2, ffn_b2):
    tok, d_model = hidden.shape
    n_heads, head_dim = cache_a.shape[3:]
    self_len, src = cache_a.shape[2], cross_a.shape[2]
    ff = ffn_w1.shape[1]
    swap = lambda arr: jnp.swapaxes(arr, 2, 3)
    sm = pl.BlockSpec(memory_space=pltpu.SMEM)
    vm = pl.BlockSpec(memory_space=VMEM)
    hbm = pl.BlockSpec(memory_space=pl.ANY)
    cache_t = jax.ShapeDtypeStruct((2, tok, n_heads, self_len, head_dim), BF16)
    n_self = tok // SELF_GROUP
    heads = VMEM((tok * HEAD_PAD, head_dim), F32)
    hid, z, out_a, out_b = pl.pallas_call(
        dense_kernel,
        out_shape=[jax.ShapeDtypeStruct((tok, d_model), F32), jax.ShapeDtypeStruct((tok, d_model), BF16), cache_t, cache_t],
        in_specs=[sm] * 2 + [vm] * 6 + [hbm] * 7,
        out_specs=[vm] * 2 + [hbm] * 2,
        scratch_shapes=[
            VMEM((12, d_model, d_model), BF16), VMEM((d_model, ff), BF16), VMEM((ff, d_model), BF16),
            VMEM((2, tok, n_heads, self_len, head_dim), BF16), VMEM((tok, 2, n_heads, src, head_dim), BF16),
            heads, heads, heads, heads, VMEM((tok, d_model), BF16),
            VMEM((HEAD_PAD, n_heads * self_len), jnp.int32), VMEM((HEAD_PAD, n_heads * src), jnp.int32),
            pltpu.SemaphoreType.DMA((12,)), pltpu.SemaphoreType.DMA((2,)), pltpu.SemaphoreType.DMA((n_self,)),
            pltpu.SemaphoreType.DMA((n_self,)), pltpu.SemaphoreType.DMA((tok,)),
        ],
        compiler_params=pltpu.CompilerParams(vmem_limit_bytes=62 * 1024 * 1024),
        name='dense_layers',
    )(self_pos, src_len, hidden, jnp.swapaxes(ln_gain, 0, 1), jnp.swapaxes(ln_shift, 0, 1), attn_b, ffn_b1.reshape(1, -1), ffn_b2.reshape(1, -1),
      swap(cache_a), swap(cross_a), swap(cache_b), swap(cross_b), attn_w, ffn_w1, ffn_w2)
    return hid, z, swap(out_a), swap(out_b)


def peer(index):
    return dict(device_id={'ep': index}, device_id_type=pl.DeviceIdType.MESH)


def neighbours():
    me = lax.axis_index('ep')
    core, x, y = me % 2, (me // 2) % 2, me // 4
    at = lambda yy, xx, cc: (yy * 2 + xx) * 2 + cc
    return me, core, x, y, at


def entry_barrier(others):
    barrier = pltpu.get_barrier_semaphore()
    for other in others:
        pl.semaphore_signal(barrier, inc=1, **peer(other))
    pl.semaphore_wait(barrier, len(others))


def gather_kernel(z_ref, ids_ref, zall_ref, idsall_ref, send_sem, recv_sem):
    me, core, x, y, at = neighbours()
    twin = at(y, x, 1 - core)
    chips = [(y, 1 - x), (1 - y, x), (1 - y, 1 - x)]
    entry_barrier([twin] + [at(cy, cx, core) for cy, cx in chips])

    def send(slot, src_z, src_ids, row, to):
        out = []
        for which, src, dst in ((0, src_z, zall_ref), (1, src_ids, idsall_ref)):
            cp = pltpu.make_async_remote_copy(
                src_ref=src, dst_ref=dst.at[row], send_sem=send_sem.at[slot, which], recv_sem=recv_sem.at[slot, which], **peer(to))
            cp.start()
            out.append(cp)
        return out

    sent = []
    for j in (2, 0, 1):
        sent.append((j, send(j, z_ref, ids_ref, me, at(*chips[j], core))))
    sent.append((3, send(3, z_ref, ids_ref, me, twin)))
    zall_ref[me] = z_ref[...]
    idsall_ref[me] = ids_ref[...]
    relays = []
    for j in (0, 1, 2):
        for cp in dict(sent)[j]:
            cp.wait_recv()
        row = at(*chips[j], core)
        relays += send(4 + j, zall_ref.at[row], idsall_ref.at[row], row, twin)
    for cp in dict(sent)[3]:
        cp.wait_recv()
    for cp in relays:
        cp.wait_recv()
    for _, cps in sent:
        for cp in cps:
            cp.wait_send()
    for cp in relays:
        cp.wait_send()


def gather_tokens(z_bf, ids_wide, group_n):
    tok, d_model = z_bf.shape
    return pl.pallas_call(
        gather_kernel,
        out_shape=[jax.ShapeDtypeStruct((group_n, tok, d_model), BF16), jax.ShapeDtypeStruct((group_n, tok, 128), jnp.int32)],
        in_specs=[pl.BlockSpec(memory_space=VMEM)] * 2,
        out_specs=[pl.BlockSpec(memory_space=VMEM)] * 2,
        scratch_shapes=[pltpu.SemaphoreType.DMA((7, 2)), pltpu.SemaphoreType.DMA((7, 2))],
        compiler_params=pltpu.CompilerParams(collective_id=0, has_side_effects=True),
        name='gather_tokens',
    )(z_bf, ids_wide)


def reduce_kernel(part_ref, hid_ref, out_ref, own, r1, s1, r2, s2, r3, send_sem, recv_sem):
    me, core, x, y, at = neighbours()
    twin, xn, yn = at(y, x, 1 - core), at(y, 1 - x, core), at(1 - y, x, core)
    entry_barrier([twin, xn, yn])
    half = hid_ref.shape[1] // 2
    cols = (pl.ds(0, half), pl.ds(half, half))

    def send(slot, src, dst, to):
        cp = pltpu.make_async_remote_copy(src_ref=src, dst_ref=dst, send_sem=send_sem.at[slot], recv_sem=recv_sem.at[slot], **peer(to))
        cp.start()
        return cp

    chips = [(1 - y, 1 - x), (y, 1 - x), (1 - y, x), (y, x)]
    first = [send(k, part_ref.at[at(cy, cx, 1 - core)], r1.at[k], twin) for k, (cy, cx) in enumerate(chips)]

    def sum1(k):
        first[k].wait_recv()
        cy, cx = chips[k]
        s1[k] = part_ref[at(cy, cx, core)] + r1[k]

    sum1(0)
    a0 = send(4, s1.at[0, :, cols[0]], r2.at[0, 0], xn)
    b0 = send(5, s1.at[0, :, cols[1]], r2.at[1, 0], yn)
    sum1(1)
    a1 = send(6, s1.at[1, :, cols[0]], r2.at[0, 1], xn)
    sum1(2)
    b1 = send(7, s1.at[2, :, cols[1]], r2.at[1, 1], yn)
    sum1(3)
    a0.wait_recv()
    s2[0] = s1[2, :, :half] + r2[0, 0]
    a2 = send(8, s2.at[0], r3.at[0], yn)
    b0.wait_recv()
    s2[1] = s1[1, :, half:] + r2[1, 0]
    b2 = send(9, s2.at[1], r3.at[1], xn)
    a1.wait_recv()
    own_a = hid_ref[:, :half] + s1[3, :, :half] + r2[0, 1]
    b1.wait_recv()
    own_b = hid_ref[:, half:] + s1[3, :, half:] + r2[1, 1]
    a2.wait_recv()
    out_ref[:, :half] = (own_a + r3[0]).astype(BF16)
    b2.wait_recv()
    out_ref[:, half:] = (own_b + r3[1]).astype(BF16)
    for cp in first + [a0, b0, a1, b1, a2, b2]:
        cp.wait_send()


def reduce_outputs(partial, hid_f32):
    group_n, tok, d_model = partial.shape
    half = d_model // 2
    return pl.pallas_call(
        reduce_kernel,
        out_shape=jax.ShapeDtypeStruct((tok, d_model), BF16),
        in_specs=[pl.BlockSpec(memory_space=VMEM)] * 2,
        out_specs=pl.BlockSpec(memory_space=VMEM),
        scratch_shapes=[
            VMEM((8, 128), F32),
            VMEM((4, tok, d_model), F32), VMEM((4, tok, d_model), F32),
            VMEM((2, 2, tok, half), F32), VMEM((2, tok, half), F32), VMEM((2, tok, half), F32),
            pltpu.SemaphoreType.DMA((10,)), pltpu.SemaphoreType.DMA((10,)),
        ],
        compiler_params=pltpu.CompilerParams(collective_id=1, has_side_effects=True),
        name='reduce_outputs',
    )(partial, hid_f32)


ROWS = 128
SPLIT = 2
SLOTS = 6


def expert_kernel(z_ref, ids_ref, rw_ref, b1_ref, b2_ref, w1_hbm, w2_hbm, out_ref,
                  w1_buf, w2_buf, rank_s, gate_s, cnt_v, cnt_s, list_s, x_s, o_s, sem1, sem2, csem):
    n_tok, d_model = z_ref.shape
    n_loc = w1_hbm.shape[0]
    ff = w1_hbm.shape[2]
    fc = ff // SPLIT
    n_blk = x_s.shape[0]
    me = lax.axis_index('ep')
    base = me * n_loc
    lane = lax.broadcasted_iota(jnp.int32, (n_tok, 128), 1)
    id0, id1 = ids_ref[:, 0:1], ids_ref[:, 1:2]
    hit_loc = jnp.logical_or(id0 - base == lane, id1 - base == lane)
    hit_loc = jnp.logical_and(hit_loc, lane < n_loc)
    hit_t = hit_loc.astype(F32)
    counts = jnp.sum(hit_t, axis=0, keepdims=True)
    cnt_v[...] = jnp.broadcast_to(counts, cnt_v.shape).astype(jnp.int32)
    cp = pltpu.make_async_copy(cnt_v, cnt_s, csem)
    cp.start()
    cp.wait()

    def scan_body(e, n_act):
        @pl.when(cnt_s[0, e] > 0)
        def _():
            list_s[n_act] = e
        return n_act + jnp.where(cnt_s[0, e] > 0, 1, 0)
    n_act = lax.fori_loop(0, n_loc, scan_body, 0)
    n_step = n_act * SPLIT

    def copies(step, slot):
        e = list_s[step // SPLIT]
        f0 = pl.multiple_of((step % SPLIT) * fc, fc)
        return (pltpu.make_async_copy(w1_hbm.at[e, :, pl.ds(f0, fc)], w1_buf.at[slot], sem1.at[slot]),
                pltpu.make_async_copy(w2_hbm.at[e, pl.ds(f0, fc), :], w2_buf.at[slot], sem2.at[slot]))

    for s in range(SLOTS):
        @pl.when(s < n_step)
        def _():
            for c in copies(s, s):
                c.start()

    hit_bf = hit_t.astype(BF16)
    row_i = lax.broadcasted_iota(jnp.int32, (n_tok, n_tok), 0)
    col_i = lax.broadcasted_iota(jnp.int32, (n_tok, n_tok), 1)
    before = (row_i < col_i).astype(BF16)
    hit = jnp.transpose(hit_t)
    rank = jnp.dot(hit.astype(BF16), before, preferred_element_type=F32)
    rank_s[...] = jnp.where(hit > 0.5, rank, -1.0)

    logits = jnp.dot(z_ref[...], rw_ref[...], preferred_element_type=F32)
    top = jnp.max(logits, axis=-1, keepdims=True)
    ex = jnp.exp(logits - top)
    probs = ex / jnp.sum(ex, axis=-1, keepdims=True)
    p0 = jnp.sum(jnp.where(lane == id0, probs, 0.0), axis=-1, keepdims=True)
    p1 = jnp.sum(jnp.where(lane == id1, probs, 0.0), axis=-1, keepdims=True)
    tot = p0 + p1
    g0, g1 = p0 / tot, p1 / tot
    gate_s[...] = jnp.where(lane == id0 - base, g0, jnp.where(lane == id1 - base, g1, 0.0))
    out_ref[...] = jnp.zeros_like(out_ref)

    def step_body(step, carry):
        slot = step % SLOTS
        e = list_s[step // SPLIT]
        part = step % SPLIT
        blocks = (cnt_s[0, e] + ROWS - 1) // ROWS
        slot_i = lax.broadcasted_iota(jnp.int32, (ROWS, n_tok), 0)

        def pick(j):
            want = (slot_i + j * ROWS).astype(F32)
            return (want == rank_s[pl.ds(e, 1), :]).astype(BF16)

        @pl.when(part == 0)
        def _():
            def gather_body(j, c):
                x_s[j] = jnp.dot(pick(j), z_ref[...], preferred_element_type=F32).astype(BF16)
                o_s[j] = jnp.broadcast_to(b2_ref[pl.ds(e, 1), :], (ROWS, d_model))
                return c
            lax.fori_loop(0, blocks, gather_body, 0)

        for c in copies(step, slot):
            c.wait()
        bias = b1_ref[pl.ds(e, 1), pl.ds(pl.multiple_of(part * fc, fc), fc)]

        def block_body(j, c):
            inner = jnp.dot(x_s[j], w1_buf[slot], preferred_element_type=F32) + bias
            inner = jnp.maximum(inner, 0.0).astype(BF16)
            o_s[j] += jnp.dot(inner, w2_buf[slot], preferred_element_type=F32)
            return c
        lax.fori_loop(0, blocks, block_body, 0)

        @pl.when(step + SLOTS < n_step)
        def _():
            for c in copies(step + SLOTS, slot):
                c.start()

        @pl.when(part == SPLIT - 1)
        def _():
            lane_g = lax.broadcasted_iota(jnp.int32, (n_tok, 128), 1)
            gate = jnp.sum(jnp.where(lane_g == e, gate_s[...], 0.0), axis=-1, keepdims=True)

            def scatter_body(j, c):
                back = lax.dot_general(pick(j), o_s[j].astype(BF16), (((0,), (0,)), ((), ())), preferred_element_type=F32)
                out_ref[...] += gate * back
                return c
            lax.fori_loop(0, blocks, scatter_body, 0)
        return carry

    lax.fori_loop(0, n_step, step_body, 0)


def run_experts(z_all, ids_all, router_w, exp_w1, exp_b1, exp_w2, exp_b2):
    n_tok, d_model = z_all.shape
    n_loc, _, ff = exp_w1.shape
    fc = ff // SPLIT
    n_blk = n_tok // ROWS
    vm = pl.BlockSpec(memory_space=VMEM)
    hbm = pl.BlockSpec(memory_space=pl.ANY)
    return pl.pallas_call(
        expert_kernel,
        out_shape=jax.ShapeDtypeStruct((n_tok, d_model), F32),
        in_specs=[vm] * 5 + [hbm] * 2,
        out_specs=vm,
        scratch_shapes=[
            VMEM((SLOTS, d_model, fc), BF16), VMEM((SLOTS, fc, d_model), BF16),
            VMEM((128, n_tok), F32), VMEM((n_tok, 128), F32),
            VMEM((8, 128), jnp.int32), pltpu.SMEM((8, 128), jnp.int32), pltpu.SMEM((n_loc,), jnp.int32),
            VMEM((n_blk, ROWS, d_model), BF16), VMEM((n_blk, ROWS, d_model), F32),
            pltpu.SemaphoreType.DMA((SLOTS,)), pltpu.SemaphoreType.DMA((SLOTS,)), pltpu.SemaphoreType.DMA,
        ],
        compiler_params=pltpu.CompilerParams(vmem_limit_bytes=60 * 1024 * 1024),
        name='run_experts',
    )(z_all, ids_all, router_w, exp_b1.astype(F32), exp_b2.astype(F32), exp_w1, exp_w2)


def solution(mesh):
    group_n = mesh.shape['ep']

    def local_step(hidden, self_pos, src_len, cache_a, cross_a, cache_b, cross_b, route_ids, ln_gain, ln_shift, attn_w, attn_b, ffn_w1, ffn_b1, ffn_w2, ffn_b2, router_w, exp_w1, exp_b1, exp_w2, exp_b2):
        hid_f32, z_bf, cache_a_new, cache_b_new = dense_layers(hidden, self_pos, src_len, cache_a, cross_a, cache_b, cross_b, ln_gain, ln_shift, attn_w, attn_b, ffn_w1, ffn_b1, ffn_w2, ffn_b2)
        tok, d_model = z_bf.shape
        ids_wide = jnp.pad(route_ids, ((0, 0), (0, 126)))
        z_all, ids_all = gather_tokens(z_bf, ids_wide, group_n)
        partial = run_experts(z_all.reshape(-1, d_model), ids_all.reshape(-1, 128), router_w, exp_w1, exp_b1, exp_w2, exp_b2)
        out = reduce_outputs(partial.reshape(group_n, tok, d_model), hid_f32)
        return out, cache_a_new, cache_b_new

    tok_spec = P(('dp', 'ep'))
    cache_spec = P(None, ('dp', 'ep'))
    rep_spec = P()
    exp_spec = P('ep')
    in_specs = (tok_spec, tok_spec, tok_spec, cache_spec, cache_spec, cache_spec, cache_spec, tok_spec) + (rep_spec,) * 9 + (exp_spec,) * 4
    out_specs = (tok_spec, cache_spec, cache_spec)
    return jax.shard_map(local_step, mesh=mesh, in_specs=in_specs, out_specs=out_specs, check_vma=False)
```

profile of v0, /device:TPU:0, one launch (start us, length us, event | category | flops | bytes accessed | tf_op | source)
XLA Modules:
  0.0 169.9 jit_solution(2115712463029841285)
XLA Ops:
  0.6 1.3 reshape.22.fb2_ref
  1.9 1.3 reshape.21.fb1_ref
  3.2 1.3 copy.24.ab_ref
  4.5 0.8 copy.25
  5.3 0.6 pad.4.ids_ref
  5.9 1.4 convert_element_type.7.b2_ref
  7.3 1.6 convert_element_type.6.b1_ref
  8.8 113.8 %dense_layers.1 = (f32[64,768]{1,0:T(8,128)}, bf16[64,768]{1,0:T(8,128)(2,1)}, bf16[2,64,12,16,64]{4,3,2,1,0:T(8,128)(2,1)}, bf16[2,64,12,16,64]{4,3,2,1,0:T(8,128)(2,1)}) custom-call(s32[64]{0:T(128)} %pos_sm.1, s32[64]{0:T(128)} %len_sm.1, bf16[64,768]{1,0:T(8,128)(2,1)} %hid_ref.1, f32[3,2,768]{2,1,0:T(2,128)} %bitcast.18, f32[3,2,768]{2,1,0:T(2,128)} %bitcast.19, ...), custom_call_target="tpu_custom_call" | custom-call | tf_op jit(solution)/shard_map/dense_layers/pallas_call | solution.py:207
  122.7 14.4 %gather_tokens.1 = (bf16[8,64,768]{2,1,0:T(8,128)(2,1)}, s32[8,64,128]{2,1,0:T(8,128)}) custom-call(bf16[64,768]{1,0:T(8,128)(2,1)} %get-tuple-element.9.z_ref, s32[64,128]{1,0:T(8,128)} %pad.4.ids_ref), custom_call_target="tpu_custom_call" | custom-call | tf_op jit(solution)/shard_map/gather_tokens/pallas_call | solution.py:285
  137.0 14.4 %run_experts.1 = f32[512,768]{1,0:T(8,128)} custom-call(bf16[512,768]{1,0:T(8,128)(2,1)} %bitcast.16, s32[512,128]{1,0:T(8,128)} %bitcast.17, bf16[768,128]{1,0:T(8,128)(2,1)} %rw_ref.1, f32[16,3072]{1,0:T(8,128)} %convert_element_type.6.b1_ref, f32[16,768]{1,0:T(8,128)} %convert_element_type.7.b2_ref, bf16[16,768,3072]{2,1,0:T(8,128)(2,1)} %w1_hbm.3, ...), custom_call_target="tpu_custom_call" | custom-call | tf_op jit(solution)/shard_map/run_experts/pallas_call | solution.py:482
  151.4 17.0 %reduce_outputs.1 = bf16[64,768]{1,0:T(8,128)(2,1)} custom-call(f32[8,64,768]{2,1,0:T(8,128)} %bitcast.13, f32[64,768]{1,0:T(8,128)} %get-tuple-element.12.hid_ref), custom_call_target="tpu_custom_call" | custom-call | tf_op jit(solution)/shard_map/reduce_outputs/pallas_call | solution.py:345
  168.4 1.5 copy.27
where the time goes:
time: 171 us; the launch traced here: 170 us
  Pallas kernels  159 us (93%)
  local copies, waits for them, and re-layouts  6.82 us (4%)
  other arithmetic  2.94 us (2%)
    pallas_call x1, Pallas kernels, dense_layers(): pl.pallas_call(dense_kernel, out_shape=[jax.ShapeDtypeStruct((tok, d_mode...  114 us
    pallas_call x1, Pallas kernels, reduce_outputs(): pl.pallas_call(reduce_kernel, out_shape=jax.ShapeDtypeStruct((tok, d_mode...  17 us
    pallas_call x1, Pallas kernels, gather_tokens(): pl.pallas_call(gather_kernel, out_shape=[jax.ShapeDtypeStruct((group_n, t...  14.4 us
    pallas_call x1, Pallas kernels, run_experts(): pl.pallas_call(expert_kernel, out_shape=jax.ShapeDtypeStruct((n_tok, d_mo...  14.4 us
    unnamed x3, local copies, waits for them, and re-layouts  3.63 us

commit v1 on v0

--- a/solution.py
+++ b/solution.py
@@ -25,10 +25,10 @@
     return (centered * lax.rsqrt(var_val + LN_EPS) * gain_vec + shift_vec).astype(BF16)
 
 
-def dense_kernel(pos_sm, len_sm, hid_ref, gain_ref, shift_ref, ab_ref, fb1_ref, fb2_ref,
+def dense_kernel(pos_sm, len_sm, pos_ref, hid_ref, gain_ref, shift_ref, ab_ref, fb1_ref, fb2_ref,
                  cache_a, cross_a, cache_b, cross_b, aw_hbm, w1_hbm, w2_hbm,
                  hid_out, z_out, cache_a_out, cache_b_out,
-                 w_buf, f1_buf, f2_buf, self_buf, cross_buf, q_s, k_s, v_s, ctx_s, cat_s, self_mask, cross_mask,
+                 w_buf, f1_buf, f2_buf, self_buf, cross_buf, q_s, k_s, v_s, ctx_s, cat_s, lim_s, self_mask, cross_mask,
                  w_sem, f_sem, in_sem, out_sem, cross_sem):
     tok, d_model = hid_ref.shape
     n_heads, self_len, head_dim = self_buf.shape[2:]
@@ -76,19 +76,22 @@
         weight_copy(i).start()
 
     def zero_tail(b, c):
-        for part in range(1, src // 16):
-            @pl.when(part * 16 >= cross_rows(b))
-            def _():
-                cross_buf[b, 1, :, part * 16:(part + 1) * 16, :] = jnp.zeros((n_heads, 16, head_dim), BF16)
-        return c
+        def zero_part(part, c2):
+            cross_buf[b, 1, :, pl.ds(pl.multiple_of(part * 16, 16), 16), :] = jnp.zeros((n_heads, 16, head_dim), BF16)
+            return c2
+        return lax.fori_loop(cross_rows(b) // 16, src // 16, zero_part, c)
     lax.fori_loop(0, tok, zero_tail, 0)
 
     def build_mask(ref, length):
         row = lax.broadcasted_iota(jnp.int32, ref.shape, 0)
         lane = lax.broadcasted_iota(jnp.int32, ref.shape, 1)
-        ref[...] = jnp.where(lane // length == row, lane % length, 1 << 20)
+        seq, head = lane // (n_heads * length), (lane // length) % n_heads
+        ref[...] = jnp.where(seq * HEAD_PAD + head == row, lane % length, 1 << 20)
     build_mask(self_mask, self_len)
     build_mask(cross_mask, src)
+    limit_col = jnp.broadcast_to(pos_ref[...] + 1, (tok, 128))
+    for hd in range(HEAD_PAD):
+        lim_s[pl.ds(hd, tok, stride=HEAD_PAD), :] = limit_col
 
     def to_heads(ref, val):
         val = val.astype(BF16).astype(F32)
@@ -101,20 +104,28 @@
             cat_s[:, h * head_dim:(h + 2) * head_dim] = jnp.concatenate(two, axis=1).astype(BF16)
         return cat_s[...]
 
-    def softmax_rows(scores, mask_ref, limit):
-        scores = jnp.where(mask_ref[...] < limit, scores * scale, -1e30)
+    def softmax_rows(scores, mask, limit):
+        scores = jnp.where(mask < limit, scores * scale, -1e30)
         top = jnp.max(scores, axis=-1, keepdims=True)
         ex = jnp.exp(scores - top)
         return (ex * (1.0 / jnp.sum(ex, axis=-1, keepdims=True))).astype(BF16)
 
-    def attend(q, keys, vals, mask_ref, limit):
-        scores = lax.dot_general(q, keys, (((1,), (1,)), ((), ())), preferred_element_type=F32)
-        probs = softmax_rows(scores, mask_ref, limit)
-        return jnp.dot(probs, vals, preferred_element_type=F32)
+    def scores_of(q, keys):
+        return lax.dot_general(q, keys, (((1,), (1,)), ((), ())), preferred_element_type=F32)
+
+    def block_diag(blocks):
+        rows = []
+        for k, blk in enumerate(blocks):
+            pad = jnp.zeros_like(blk)
+            rows.append(jnp.concatenate([blk if j == k else pad for j in range(len(blocks))], axis=1))
+        return jnp.concatenate(rows, axis=0)
+
+    def head_rows(b, n):
+        return pl.ds(pl.multiple_of(b * HEAD_PAD, HEAD_PAD), n * HEAD_PAD)
 
     def proj(layer, i, x_bf):
         weight_copy(layer * 6 + i).wait()
-        bias = ab_ref[layer, i:i + 1, :].astype(F32)
+        bias = ab_ref[i].astype(F32)[layer:layer + 1, :]
         return jnp.dot(x_bf, w_buf[layer * 6 + i], preferred_element_type=F32) + bias
 
     def self_layer(layer, h, cache, cache_out):
@@ -126,20 +137,28 @@
 
         def body(g, c):
             self_in(cache, g).wait()
-            for u in range(SELF_GROUP):
-                b = g * SELF_GROUP + u
-                hit = row_i == pos_sm[b]
-                kv = []
-                for which, new in ((0, k_s), (1, v_s)):
-                    tiles = []
+            sides = []
+            for which, new in ((0, k_s), (1, v_s)):
+                tiles = []
+                for u in range(SELF_GROUP):
+                    b = g * SELF_GROUP + u
+                    hit = row_i == pos_sm[b]
                     for hd in range(n_heads):
                         row = new[pl.ds(b * HEAD_PAD + hd, self_len, stride=0), :]
                         tile = jnp.where(hit, row, self_buf[which, b, hd].astype(F32)).astype(BF16)
                         self_buf[which, b, hd] = tile
                         tiles.append(tile)
-                    kv.append(jnp.concatenate(tiles, axis=0))
-                q = q_s[pl.ds(pl.multiple_of(b * HEAD_PAD, HEAD_PAD), HEAD_PAD), :].astype(BF16)
-                ctx_s[pl.ds(pl.multiple_of(b * HEAD_PAD, HEAD_PAD), HEAD_PAD), :] = attend(q, kv[0], kv[1], self_mask, pos_sm[b] + 1)
+                sides.append(jnp.concatenate(tiles, axis=0))
+                if which == 0:
+                    q = q_s[head_rows(g * SELF_GROUP, SELF_GROUP), :].astype(BF16)
+                    scores = scores_of(q, sides[0])
+            two = 2 * n_heads * self_len
+            blocks = []
+            for p in range(SELF_GROUP // 2):
+                lim = lim_s[head_rows(g * SELF_GROUP + 2 * p, 2), :]
+                lim = jnp.concatenate([lim] * (two // 128), axis=1)
+                blocks.append(softmax_rows(scores[p * 2 * HEAD_PAD:(p + 1) * 2 * HEAD_PAD, p * two:(p + 1) * two], self_mask[...], lim))
+            ctx_s[head_rows(g * SELF_GROUP, SELF_GROUP), :] = jnp.dot(block_diag(blocks), sides[1], preferred_element_type=F32)
             self_out(cache_out, g).start()
             return c
         lax.fori_loop(0, n_self, body, 0)
@@ -151,20 +170,24 @@
         to_heads(q_s, proj(layer, 4, x))
 
         def body(g, c):
-            for u in range(GROUP):
-                cross_copy(cross, g * GROUP + u).wait()
-            for u in range(GROUP):
-                b = g * GROUP + u
-                rows = pl.ds(pl.multiple_of(b * HEAD_PAD, HEAD_PAD), HEAD_PAD)
-                q = q_s[rows, :].astype(BF16)
-                keys = cross_buf[b, 0].reshape(n_heads * src, head_dim)
-                vals = cross_buf[b, 1].reshape(n_heads * src, head_dim)
-                ctx_s[rows, :] = attend(q, keys, vals, cross_mask, len_sm[b])
+            first = g * (2 * GROUP)
+            for u in range(2 * GROUP):
+                cross_copy(cross, first + u).wait()
+            halves = [first, first + GROUP]
+            scores = []
+            for at in halves:
+                q = q_s[head_rows(at, GROUP), :].astype(BF16)
+                scores.append(scores_of(q, cross_buf[pl.ds(at, GROUP), 0].reshape(GROUP * n_heads * src, head_dim)))
+            wide = n_heads * src
+            for at, sc in zip(halves, scores):
+                blocks = [softmax_rows(sc[u * HEAD_PAD:(u + 1) * HEAD_PAD, u * wide:(u + 1) * wide], cross_mask[...], len_sm[at + u]) for u in range(GROUP)]
+                vals = cross_buf[pl.ds(at, GROUP), 1].reshape(GROUP * wide, head_dim)
+                ctx_s[head_rows(at, GROUP), :] = jnp.dot(block_diag(blocks), vals, preferred_element_type=F32)
             if after is not None:
-                for u in range(GROUP):
-                    cross_copy(after, g * GROUP + u).start()
+                for u in range(2 * GROUP):
+                    cross_copy(after, first + u).start()
             return c
-        lax.fori_loop(0, tok // GROUP, body, 0)
+        lax.fori_loop(0, tok // (2 * GROUP), body, 0)
         ctx = from_heads(ctx_s)
         return h + proj(layer, 5, ctx)
 
@@ -178,9 +201,9 @@
     x = norm_rows(h, gain_ref[2, 0:1, :], shift_ref[2, 0:1, :])
     for cp in ffn_copies():
         cp.wait()
-    acc = h + fb2_ref[...].astype(F32)
+    acc = h + fb2_ref[...].astype(F32).reshape(1, d_model)
     for f in range(0, ff, d_model):
-        inner = jnp.dot(x, f1_buf[:, f:f + d_model], preferred_element_type=F32) + fb1_ref[:, f:f + d_model].astype(F32)
+        inner = jnp.dot(x, f1_buf[:, f:f + d_model], preferred_element_type=F32) + fb1_ref[f:f + d_model].astype(F32).reshape(1, d_model)
         inner = jnp.maximum(inner, 0.0).astype(BF16)
         acc = acc + jnp.dot(inner, f2_buf[f:f + d_model, :], preferred_element_type=F32)
     h = acc
@@ -207,19 +230,19 @@
     hid, z, out_a, out_b = pl.pallas_call(
         dense_kernel,
         out_shape=[jax.ShapeDtypeStruct((tok, d_model), F32), jax.ShapeDtypeStruct((tok, d_model), BF16), cache_t, cache_t],
-        in_specs=[sm] * 2 + [vm] * 6 + [hbm] * 7,
+        in_specs=[sm] * 2 + [vm] * 7 + [hbm] * 7,
         out_specs=[vm] * 2 + [hbm] * 2,
         scratch_shapes=[
             VMEM((12, d_model, d_model), BF16), VMEM((d_model, ff), BF16), VMEM((ff, d_model), BF16),
             VMEM((2, tok, n_heads, self_len, head_dim), BF16), VMEM((tok, 2, n_heads, src, head_dim), BF16),
-            heads, heads, heads, heads, VMEM((tok, d_model), BF16),
-            VMEM((HEAD_PAD, n_heads * self_len), jnp.int32), VMEM((HEAD_PAD, n_heads * src), jnp.int32),
+            heads, heads, heads, heads, VMEM((tok, d_model), BF16), VMEM((tok * HEAD_PAD, 128), jnp.int32),
+            VMEM((2 * HEAD_PAD, 2 * n_heads * self_len), jnp.int32), VMEM((HEAD_PAD, n_heads * src), jnp.int32),
             pltpu.SemaphoreType.DMA((12,)), pltpu.SemaphoreType.DMA((2,)), pltpu.SemaphoreType.DMA((n_self,)),
             pltpu.SemaphoreType.DMA((n_self,)), pltpu.SemaphoreType.DMA((tok,)),
         ],
         compiler_params=pltpu.CompilerParams(vmem_limit_bytes=62 * 1024 * 1024),
         name='dense_layers',
-    )(self_pos, src_len, hidden, jnp.swapaxes(ln_gain, 0, 1), jnp.swapaxes(ln_shift, 0, 1), attn_b, ffn_b1.reshape(1, -1), ffn_b2.reshape(1, -1),
+    )(self_pos, src_len, self_pos.reshape(-1, 1), hidden, jnp.swapaxes(ln_gain, 0, 1), jnp.swapaxes(ln_shift, 0, 1), jnp.swapaxes(attn_b, 0, 1), ffn_b1, ffn_b2,
       swap(cache_a), swap(cross_a), swap(cache_b), swap(cross_b), attn_w, ffn_w1, ffn_w2)
     return hid, z, swap(out_a), swap(out_b)
 
@@ -242,10 +265,14 @@
     pl.semaphore_wait(barrier, len(others))
 
 
-def gather_kernel(z_ref, ids_ref, zall_ref, idsall_ref, send_sem, recv_sem):
+def gather_kernel(z_ref, idst_ref, zall_ref, idsall_ref, flip, ids_ref, send_sem, recv_sem):
     me, core, x, y, at = neighbours()
     twin = at(y, x, 1 - core)
     chips = [(y, 1 - x), (1 - y, x), (1 - y, 1 - x)]
+    tok = z_ref.shape[0]
+    flip[...] = jnp.zeros_like(flip)
+    flip[0:2, 0:tok] = idst_ref[...].astype(F32)
+    ids_ref[...] = jnp.transpose(flip[...])[:tok]
     entry_barrier([twin] + [at(cy, cx, core) for cy, cx in chips])
 
     def send(slot, src_z, src_ids, row, to):
@@ -280,17 +307,17 @@
         cp.wait_send()
 
 
-def gather_tokens(z_bf, ids_wide, group_n):
+def gather_tokens(z_bf, ids_t, group_n):
     tok, d_model = z_bf.shape
     return pl.pallas_call(
         gather_kernel,
-        out_shape=[jax.ShapeDtypeStruct((group_n, tok, d_model), BF16), jax.ShapeDtypeStruct((group_n, tok, 128), jnp.int32)],
+        out_shape=[jax.ShapeDtypeStruct((group_n, tok, d_model), BF16), jax.ShapeDtypeStruct((group_n, tok, 128), F32)],
         in_specs=[pl.BlockSpec(memory_space=VMEM)] * 2,
         out_specs=[pl.BlockSpec(memory_space=VMEM)] * 2,
-        scratch_shapes=[pltpu.SemaphoreType.DMA((7, 2)), pltpu.SemaphoreType.DMA((7, 2))],
+        scratch_shapes=[VMEM((128, 128), F32), VMEM((tok, 128), F32), pltpu.SemaphoreType.DMA((7, 2)), pltpu.SemaphoreType.DMA((7, 2))],
         compiler_params=pltpu.CompilerParams(collective_id=0, has_side_effects=True),
         name='gather_tokens',
-    )(z_bf, ids_wide)
+    )(z_bf, ids_t)
 
 
 def reduce_kernel(part_ref, hid_ref, out_ref, own, r1, s1, r2, s2, r3, send_sem, recv_sem):
@@ -363,8 +390,8 @@
 SLOTS = 6
 
 
-def expert_kernel(z_ref, ids_ref, rw_ref, b1_ref, b2_ref, w1_hbm, w2_hbm, out_ref,
-                  w1_buf, w2_buf, rank_s, gate_s, cnt_v, cnt_s, list_s, x_s, o_s, sem1, sem2, csem):
+def expert_kernel(z_ref, ids_ref, rw_ref, b1_in, b2_in, w1_hbm, w2_hbm, out_ref,
+                  b1_ref, b2_ref, w1_buf, w2_buf, rank_s, gate_s, cnt_v, cnt_s, list_s, x_s, o_s, sem1, sem2, csem):
     n_tok, d_model = z_ref.shape
     n_loc = w1_hbm.shape[0]
     ff = w1_hbm.shape[2]
@@ -373,7 +400,7 @@
     me = lax.axis_index('ep')
     base = me * n_loc
     lane = lax.broadcasted_iota(jnp.int32, (n_tok, 128), 1)
-    id0, id1 = ids_ref[:, 0:1], ids_ref[:, 1:2]
+    id0, id1 = ids_ref[:, 0:1].astype(jnp.int32), ids_ref[:, 1:2].astype(jnp.int32)
     hit_loc = jnp.logical_or(id0 - base == lane, id1 - base == lane)
     hit_loc = jnp.logical_and(hit_loc, lane < n_loc)
     hit_t = hit_loc.astype(F32)
@@ -403,6 +430,8 @@
             for c in copies(s, s):
                 c.start()
 
+    b1_ref[...] = b1_in[...].astype(F32)
+    b2_ref[...] = b2_in[...].astype(F32)
     hit_bf = hit_t.astype(BF16)
     row_i = lax.broadcasted_iota(jnp.int32, (n_tok, n_tok), 0)
     col_i = lax.broadcasted_iota(jnp.int32, (n_tok, n_tok), 1)
@@ -485,6 +514,7 @@
         in_specs=[vm] * 5 + [hbm] * 2,
         out_specs=vm,
         scratch_shapes=[
+            VMEM((n_loc, ff), F32), VMEM((n_loc, d_model), F32),
             VMEM((SLOTS, d_model, fc), BF16), VMEM((SLOTS, fc, d_model), BF16),
             VMEM((128, n_tok), F32), VMEM((n_tok, 128), F32),
             VMEM((8, 128), jnp.int32), pltpu.SMEM((8, 128), jnp.int32), pltpu.SMEM((n_loc,), jnp.int32),
@@ -493,7 +523,7 @@
         ],
         compiler_params=pltpu.CompilerParams(vmem_limit_bytes=60 * 1024 * 1024),
         name='run_experts',
-    )(z_all, ids_all, router_w, exp_b1.astype(F32), exp_b2.astype(F32), exp_w1, exp_w2)
+    )(z_all, ids_all, router_w, exp_b1, exp_b2, exp_w1, exp_w2)
 
 
 def solution(mesh):
@@ -502,8 +532,7 @@
     def local_step(hidden, self_pos, src_len, cache_a, cross_a, cache_b, cross_b, route_ids, ln_gain, ln_shift, attn_w, attn_b, ffn_w1, ffn_b1, ffn_w2, ffn_b2, router_w, exp_w1, exp_b1, exp_w2, exp_b2):
         hid_f32, z_bf, cache_a_new, cache_b_new = dense_layers(hidden, self_pos, src_len, cache_a, cross_a, cache_b, cross_b, ln_gain, ln_shift, attn_w, attn_b, ffn_w1, ffn_b1, ffn_w2, ffn_b2)
         tok, d_model = z_bf.shape
-        ids_wide = jnp.pad(route_ids, ((0, 0), (0, 126)))
-        z_all, ids_all = gather_tokens(z_bf, ids_wide, group_n)
+        z_all, ids_all = gather_tokens(z_bf, route_ids.T, group_n)
         partial = run_experts(z_all.reshape(-1, d_model), ids_all.reshape(-1, 128), router_w, exp_w1, exp_b1, exp_w2, exp_b2)
         out = reduce_outputs(partial.reshape(group_n, tok, d_model), hid_f32)
         return out, cache_a_new, cache_b_new

time: 171 us -> 94.8 us (0.55)
  Pallas kernels: 159 us -> 90.8 us
  local copies, waits for them, and re-layouts: 6.82 us -> 2.89 us
  other arithmetic: 2.94 us -> 0 us
    pallas_call x1, Pallas kernels: 114 us -> 44.1 us  [dense_layers(): pl.pallas_call(dense_kernel, out_shape=[jax.ShapeDtypeStruct((tok, d_mode...]
    pallas_call x1, Pallas kernels: 14.4 us -> 20 us  [run_experts(): pl.pallas_call(expert_kernel, out_shape=jax.ShapeDtypeStruct((n_tok, d_mo...]
    pallas_call x1, Pallas kernels: 17 us -> 12.2 us  [reduce_outputs(): pl.pallas_call(reduce_kernel, out_shape=jax.ShapeDtypeStruct((tok, d_mode...]
    convert_element_type x2 -> x0, other arithmetic: 2.94 us -> none  [the longest x1 1.58 us: run_experts(): exp_b1.astype(F32)]
    unnamed x3 -> x1, local copies, waits for them, and re-layouts: 3.63 us -> 1.54 us
where the time goes in v1:
time: 94.8 us; the launch traced here: 94.3 us
  Pallas kernels  90.8 us (96%)
  local copies, waits for them, and re-layouts  2.89 us (3%)
    pallas_call x1, Pallas kernels, dense_layers(): pl.pallas_call(dense_kernel, out_shape=[jax.ShapeDtypeStruct((tok, d_mode...  44.1 us
    pallas_call x1, Pallas kernels, run_experts(): pl.pallas_call(expert_kernel, out_shape=jax.ShapeDtypeStruct((n_tok, d_mo...  20 us
    pallas_call x1, Pallas kernels, gather_tokens(): pl.pallas_call(gather_kernel, out_shape=[jax.ShapeDtypeStruct((group_n, t...  14.6 us
    pallas_call x1, Pallas kernels, reduce_outputs(): pl.pallas_call(reduce_kernel, out_shape=jax.ShapeDtypeStruct((tok, d_mode...  12.2 us

profile of v1, /device:TPU:0, one launch (start us, length us, event | category | flops | bytes accessed | tf_op | source)
XLA Modules:
  0.0 94.3 jit_solution(17801990349255916678)
XLA Ops:
  0.6 1.3 %copy.24.pos_ref = s32[64,1]{1,0:T(8,128)} copy(s32[64,1]{0,1:T(1,128)} %bitcast.24) | data formatting | bytes 512 | tf_op jit(solution)/shard_map/reshape | solution.py:245
  2.0 44.1 %dense_layers.1 = (f32[64,768]{1,0:T(8,128)}, bf16[64,768]{1,0:T(8,128)(2,1)}, bf16[2,64,12,16,64]{4,3,2,1,0:T(8,128)(2,1)}, bf16[2,64,12,16,64]{4,3,2,1,0:T(8,128)(2,1)}) custom-call(s32[64]{0:T(128)} %pos_sm.1, s32[64]{0:T(128)} %len_sm.1, s32[64,1]{1,0:T(8,128)} %copy.24.pos_ref, bf16[64,768]{1,0:T(8,128)(2,1)} %hid_ref.1, f32[3,2,768]{2,1,0:T(2,128)} %bitcast.21, ...), custom_call_target="tpu_custom_call" | custom-call | tf_op jit(solution)/shard_map/dense_layers/pallas_call | solution.py:230
  46.1 14.6 %gather_tokens.1 = (bf16[8,64,768]{2,1,0:T(8,128)(2,1)}, f32[8,64,128]{2,1,0:T(8,128)}) custom-call(bf16[64,768]{1,0:T(8,128)(2,1)} %get-tuple-element.9.z_ref, s32[2,64]{1,0:T(2,128)} %bitcast.25), custom_call_target="tpu_custom_call" | custom-call | tf_op jit(solution)/shard_map/gather_tokens/pallas_call | solution.py:312
  60.7 20.0 %run_experts.1 = f32[512,768]{1,0:T(8,128)} custom-call(bf16[512,768]{1,0:T(8,128)(2,1)} %bitcast.19, f32[512,128]{1,0:T(8,128)} %bitcast.20, bf16[768,128]{1,0:T(8,128)(2,1)} %rw_ref.1, bf16[16,3072]{1,0:T(8,128)(2,1)} %b1_in.1, bf16[16,768]{1,0:T(8,128)(2,1)} %b2_in.1, bf16[16,768,3072]{2,1,0:T(8,128)(2,1)} %w1_hbm.3, bf16[16,3072,768]{2,1,0:T(8,128)(2,1)} %w2_hbm.3), custom_call_target="tpu_custom_call" | custom-call | tf_op jit(solution)/shard_map/run_experts/pallas_call | solution.py:511
  80.6 12.2 %reduce_outputs.1 = bf16[64,768]{1,0:T(8,128)(2,1)} custom-call(f32[8,64,768]{2,1,0:T(8,128)} %bitcast.16, f32[64,768]{1,0:T(8,128)} %get-tuple-element.12.hid_ref), custom_call_target="tpu_custom_call" | custom-call | tf_op jit(solution)/shard_map/reduce_outputs/pallas_call | solution.py:372
  92.8 1.5 %copy.26 = bf16[64,768]{1,0:T(8,128)(2,1)} copy(bf16[64,768]{1,0:T(8,128)(2,1)} %reduce_outputs.1) | data formatting | bytes 196608

commit v2 on v1

--- a/solution.py
+++ b/solution.py
@@ -13,8 +13,10 @@
 VMEM = pltpu.VMEM
 
 
-GROUP = 4
-SELF_GROUP = 8
+CROSS_GROUP = 16
+CROSS_UNIT = 1
+SELF_GROUP = 16
+SELF_UNIT = 2
 HEAD_PAD = 16
 
 
@@ -25,7 +27,7 @@
     return (centered * lax.rsqrt(var_val + LN_EPS) * gain_vec + shift_vec).astype(BF16)
 
 
-def dense_kernel(pos_sm, len_sm, pos_ref, hid_ref, gain_ref, shift_ref, ab_ref, fb1_ref, fb2_ref,
+def dense_kernel(pos_sm, len_sm, hid_ref, gain_ref, shift_ref, ab_ref, fb1_ref, fb2_ref,
                  cache_a, cross_a, cache_b, cross_b, aw_hbm, w1_hbm, w2_hbm,
                  hid_out, z_out, cache_a_out, cache_b_out,
                  w_buf, f1_buf, f2_buf, self_buf, cross_buf, q_s, k_s, v_s, ctx_s, cat_s, lim_s, self_mask, cross_mask,
@@ -37,6 +39,9 @@
     scale = head_dim ** -0.5
     n_self = tok // SELF_GROUP
 
+    def head_rows(b, n):
+        return pl.ds(pl.multiple_of(b * HEAD_PAD, HEAD_PAD), n * HEAD_PAD)
+
     def weight_copy(i):
         return pltpu.make_async_copy(aw_hbm.at[i // 6, i % 6], w_buf.at[i], w_sem.at[i])
 
@@ -89,9 +94,11 @@
         ref[...] = jnp.where(seq * HEAD_PAD + head == row, lane % length, 1 << 20)
     build_mask(self_mask, self_len)
     build_mask(cross_mask, src)
-    limit_col = jnp.broadcast_to(pos_ref[...] + 1, (tok, 128))
-    for hd in range(HEAD_PAD):
-        lim_s[pl.ds(hd, tok, stride=HEAD_PAD), :] = limit_col
+
+    def fill_limit(b, c):
+        lim_s[head_rows(b, 1), :] = jnp.full((HEAD_PAD, 128), pos_sm[b] + 1, jnp.int32)
+        return c
+    lax.fori_loop(0, tok, fill_limit, 0)
 
     def to_heads(ref, val):
         val = val.astype(BF16).astype(F32)
@@ -120,9 +127,6 @@
             rows.append(jnp.concatenate([blk if j == k else pad for j in range(len(blocks))], axis=1))
         return jnp.concatenate(rows, axis=0)
 
-    def head_rows(b, n):
-        return pl.ds(pl.multiple_of(b * HEAD_PAD, HEAD_PAD), n * HEAD_PAD)
-
     def proj(layer, i, x_bf):
         weight_copy(layer * 6 + i).wait()
         bias = ab_ref[i].astype(F32)[layer:layer + 1, :]
@@ -134,31 +138,39 @@
         to_heads(k_s, proj(layer, 1, x))
         to_heads(v_s, proj(layer, 2, x))
         row_i = lax.broadcasted_iota(jnp.int32, (self_len, head_dim), 0)
+        row_b = row_i.astype(F32).astype(BF16)
 
         def body(g, c):
             self_in(cache, g).wait()
+            first = g * SELF_GROUP
             sides = []
             for which, new in ((0, k_s), (1, v_s)):
                 tiles = []
                 for u in range(SELF_GROUP):
-                    b = g * SELF_GROUP + u
-                    hit = row_i == pos_sm[b]
+                    b = first + u
+                    hit = row_b == jnp.full(row_b.shape, pos_sm[b], jnp.int32).astype(F32).astype(BF16)
                     for hd in range(n_heads):
                         row = new[pl.ds(b * HEAD_PAD + hd, self_len, stride=0), :]
-                        tile = jnp.where(hit, row, self_buf[which, b, hd].astype(F32)).astype(BF16)
+                        tile = jnp.where(hit, row.astype(BF16), self_buf[which, b, hd])
                         self_buf[which, b, hd] = tile
                         tiles.append(tile)
-                sides.append(jnp.concatenate(tiles, axis=0))
-                if which == 0:
-                    q = q_s[head_rows(g * SELF_GROUP, SELF_GROUP), :].astype(BF16)
-                    scores = scores_of(q, sides[0])
-            two = 2 * n_heads * self_len
-            blocks = []
-            for p in range(SELF_GROUP // 2):
-                lim = lim_s[head_rows(g * SELF_GROUP + 2 * p, 2), :]
-                lim = jnp.concatenate([lim] * (two // 128), axis=1)
-                blocks.append(softmax_rows(scores[p * 2 * HEAD_PAD:(p + 1) * 2 * HEAD_PAD, p * two:(p + 1) * two], self_mask[...], lim))
-            ctx_s[head_rows(g * SELF_GROUP, SELF_GROUP), :] = jnp.dot(block_diag(blocks), sides[1], preferred_element_type=F32)
+                sides.append(tiles)
+            n = SELF_UNIT
+            parts = range(0, SELF_GROUP, n)
+            wide = n * n_heads * self_len
+            stack = lambda tiles, p: jnp.concatenate(tiles[p * n_heads:(p + n) * n_heads], axis=0)
+            scores = [scores_of(q_s[head_rows(first + p, n), :].astype(BF16), stack(sides[0], p)) for p in parts]
+            probs = []
+            for p, sc in zip(parts, scores):
+                two = 2 * n_heads * self_len
+                blocks = []
+                for k in range(n // 2):
+                    lim = lim_s[head_rows(first + p + 2 * k, 2), :]
+                    lim = jnp.concatenate([lim] * (two // 128), axis=1)
+                    blocks.append(softmax_rows(sc[k * 2 * HEAD_PAD:(k + 1) * 2 * HEAD_PAD, k * two:(k + 1) * two], self_mask[...], lim))
+                probs.append(block_diag(blocks))
+            for p, pr in zip(parts, probs):
+                ctx_s[head_rows(first + p, n), :] = jnp.dot(pr, stack(sides[1], p), preferred_element_type=F32)
             self_out(cache_out, g).start()
             return c
         lax.fori_loop(0, n_self, body, 0)
@@ -170,24 +182,24 @@
         to_heads(q_s, proj(layer, 4, x))
 
         def body(g, c):
-            first = g * (2 * GROUP)
-            for u in range(2 * GROUP):
+            first = g * CROSS_GROUP
+            for u in range(CROSS_GROUP):
                 cross_copy(cross, first + u).wait()
-            halves = [first, first + GROUP]
-            scores = []
-            for at in halves:
-                q = q_s[head_rows(at, GROUP), :].astype(BF16)
-                scores.append(scores_of(q, cross_buf[pl.ds(at, GROUP), 0].reshape(GROUP * n_heads * src, head_dim)))
+            n = CROSS_UNIT
+            parts = [first + p for p in range(0, CROSS_GROUP, n)]
             wide = n_heads * src
-            for at, sc in zip(halves, scores):
-                blocks = [softmax_rows(sc[u * HEAD_PAD:(u + 1) * HEAD_PAD, u * wide:(u + 1) * wide], cross_mask[...], len_sm[at + u]) for u in range(GROUP)]
-                vals = cross_buf[pl.ds(at, GROUP), 1].reshape(GROUP * wide, head_dim)
-                ctx_s[head_rows(at, GROUP), :] = jnp.dot(block_diag(blocks), vals, preferred_element_type=F32)
+            scores = [scores_of(q_s[head_rows(at, n), :].astype(BF16), cross_buf[pl.ds(at, n), 0].reshape(n * wide, head_dim)) for at in parts]
+            probs = []
+            for at, sc in zip(parts, scores):
+                probs.append(block_diag([softmax_rows(sc[u * HEAD_PAD:(u + 1) * HEAD_PAD, u * wide:(u + 1) * wide], cross_mask[...], len_sm[at + u]) for u in range(n)]))
+            for at, pr in zip(parts, probs):
+                vals = cross_buf[pl.ds(at, n), 1].reshape(n * wide, head_dim)
+                ctx_s[head_rows(at, n), :] = jnp.dot(pr, vals, preferred_element_type=F32)
             if after is not None:
-                for u in range(2 * GROUP):
+                for u in range(CROSS_GROUP):
                     cross_copy(after, first + u).start()
             return c
-        lax.fori_loop(0, tok // (2 * GROUP), body, 0)
+        lax.fori_loop(0, tok // CROSS_GROUP, body, 0)
         ctx = from_heads(ctx_s)
         return h + proj(layer, 5, ctx)
 
@@ -229,8 +241,8 @@
     heads = VMEM((tok * HEAD_PAD, head_dim), F32)
     hid, z, out_a, out_b = pl.pallas_call(
         dense_kernel,
-        out_shape=[jax.ShapeDtypeStruct((tok, d_model), F32), jax.ShapeDtypeStruct((tok, d_model), BF16), cache_t, cache_t],
-        in_specs=[sm] * 2 + [vm] * 7 + [hbm] * 7,
+        out_shape=[VMEM((tok, d_model), F32), VMEM((tok, d_model), BF16), cache_t, cache_t],
+        in_specs=[sm] * 2 + [vm] * 6 + [hbm] * 7,
         out_specs=[vm] * 2 + [hbm] * 2,
         scratch_shapes=[
             VMEM((12, d_model, d_model), BF16), VMEM((d_model, ff), BF16), VMEM((ff, d_model), BF16),
@@ -240,9 +252,9 @@
             pltpu.SemaphoreType.DMA((12,)), pltpu.SemaphoreType.DMA((2,)), pltpu.SemaphoreType.DMA((n_self,)),
             pltpu.SemaphoreType.DMA((n_self,)), pltpu.SemaphoreType.DMA((tok,)),
         ],
-        compiler_params=pltpu.CompilerParams(vmem_limit_bytes=62 * 1024 * 1024),
+        compiler_params=pltpu.CompilerParams(vmem_limit_bytes=61 * 1024 * 1024),
         name='dense_layers',
-    )(self_pos, src_len, self_pos.reshape(-1, 1), hidden, jnp.swapaxes(ln_gain, 0, 1), jnp.swapaxes(ln_shift, 0, 1), jnp.swapaxes(attn_b, 0, 1), ffn_b1, ffn_b2,
+    )(self_pos, src_len, hidden, jnp.swapaxes(ln_gain, 0, 1), jnp.swapaxes(ln_shift, 0, 1), jnp.swapaxes(attn_b, 0, 1), ffn_b1, ffn_b2,
       swap(cache_a), swap(cross_a), swap(cache_b), swap(cross_b), attn_w, ffn_w1, ffn_w2)
     return hid, z, swap(out_a), swap(out_b)
 
@@ -265,62 +277,96 @@
     pl.semaphore_wait(barrier, len(others))
 
 
-def gather_kernel(z_ref, idst_ref, zall_ref, idsall_ref, flip, ids_ref, send_sem, recv_sem):
+def named_experts(ids_cols, base, n_loc):
+    n_tok = ids_cols.shape[0]
+    lane = lax.broadcasted_iota(jnp.int32, (n_tok, 128), 1)
+    id0 = ids_cols[:, 0:1].astype(jnp.int32) - base
+    id1 = ids_cols[:, 1:2].astype(jnp.int32) - base
+    hit = jnp.logical_and(jnp.logical_or(id0 == lane, id1 == lane), lane < n_loc)
+    return id0, id1, lane, hit.astype(F32)
+
+
+def gather_kernel(n_loc, z_ref, idst_ref, zall_ref, cols_ref, meta_ref, flip, ids_ref, idsall, send_sem, recv_sem):
     me, core, x, y, at = neighbours()
     twin = at(y, x, 1 - core)
     chips = [(y, 1 - x), (1 - y, x), (1 - y, 1 - x)]
     tok = z_ref.shape[0]
-    flip[...] = jnp.zeros_like(flip)
-    flip[0:2, 0:tok] = idst_ref[...].astype(F32)
-    ids_ref[...] = jnp.transpose(flip[...])[:tok]
+    group_n = zall_ref.shape[0]
+    ids_ref[...] = jnp.zeros_like(ids_ref)
+    ids_ref[0:2, 0:tok] = idst_ref[...].astype(F32)
     entry_barrier([twin] + [at(cy, cx, core) for cy, cx in chips])
 
-    def send(slot, src_z, src_ids, row, to):
-        out = []
-        for which, src, dst in ((0, src_z, zall_ref), (1, src_ids, idsall_ref)):
-            cp = pltpu.make_async_remote_copy(
-                src_ref=src, dst_ref=dst.at[row], send_sem=send_sem.at[slot, which], recv_sem=recv_sem.at[slot, which], **peer(to))
-            cp.start()
-            out.append(cp)
-        return out
-
-    sent = []
-    for j in (2, 0, 1):
-        sent.append((j, send(j, z_ref, ids_ref, me, at(*chips[j], core))))
-    sent.append((3, send(3, z_ref, ids_ref, me, twin)))
+    def send(slot, which, src, row, to):
+        dst = (idsall, zall_ref)[which]
+        cp = pltpu.make_async_remote_copy(
+            src_ref=src, dst_ref=dst.at[row], send_sem=send_sem.at[slot, which], recv_sem=recv_sem.at[slot, which], **peer(to))
+        cp.start()
+        return cp
+
+    far = [at(cy, cx, core) for cy, cx in chips]
+    ids_sent = [send(j, 0, ids_ref, me, far[j]) for j in range(3)] + [send(3, 0, ids_ref, me, twin)]
+    z_sent = {j: send(j, 1, z_ref, me, far[j]) for j in (2, 0, 1)}
+    z_sent[3] = send(3, 1, z_ref, me, twin)
     zall_ref[me] = z_ref[...]
-    idsall_ref[me] = ids_ref[...]
+    idsall[me] = ids_ref[...]
     relays = []
-    for j in (0, 1, 2):
-        for cp in dict(sent)[j]:
-            cp.wait_recv()
-        row = at(*chips[j], core)
-        relays += send(4 + j, zall_ref.at[row], idsall_ref.at[row], row, twin)
-    for cp in dict(sent)[3]:
-        cp.wait_recv()
+    for j in range(3):
+        ids_sent[j].wait_recv()
+        relays.append(send(4 + j, 0, idsall.at[far[j]], far[j], twin))
+    ids_sent[3].wait_recv()
     for cp in relays:
         cp.wait_recv()
-    for _, cps in sent:
-        for cp in cps:
-            cp.wait_send()
-    for cp in relays:
+
+    flip[...] = jnp.zeros_like(flip)
+    for d in range(group_n):
+        flip[2 * d:2 * d + 2, :] = idsall[d, 0:2, :]
+    cols = jnp.transpose(flip[...])[:tok]
+    lane_b = lax.broadcasted_iota(jnp.int32, (tok, 128), 1)
+    wide = [jnp.where(lane_b == 0, cols[:, 2 * d:2 * d + 1], cols[:, 2 * d + 1:2 * d + 2]) for d in range(group_n)]
+    cols_ref[...] = jnp.concatenate(wide, axis=0)
+    _, _, _, hit = named_experts(cols_ref[...], me * n_loc, n_loc)
+    ones = jnp.ones((group_n * tok, 128), BF16)
+    count = lax.dot_general(hit.astype(BF16), ones, (((0,), (0,)), ((), ())), preferred_element_type=F32)
+    row_i = lax.broadcasted_iota(jnp.int32, (128, 128), 0)
+    col_i = lax.broadcasted_iota(jnp.int32, (128, 128), 1)
+    named = (count > 0.5).astype(F32)
+    order = jnp.dot((row_i > col_i).astype(BF16), named.astype(BF16), preferred_element_type=F32)
+    spot = jnp.where(order == col_i.astype(F32), named, 0.0)
+    expert_list = jnp.sum(spot * row_i.astype(F32), axis=0, keepdims=True)
+    counts = jnp.sum(hit, axis=0, keepdims=True)
+    total = jnp.sum(named, axis=0, keepdims=True)
+    meta_ref[...] = jnp.concatenate([counts, expert_list, total, jnp.zeros((5, 128), F32)], axis=0).astype(jnp.int32)
+
+    z_relays = []
+    for j in (0, 1, 2):
+        z_sent[j].wait_recv()
+        z_relays.append(send(4 + j, 1, zall_ref.at[far[j]], far[j], twin))
+    z_sent[3].wait_recv()
+    for cp in z_relays:
+        cp.wait_recv()
+    for cp in ids_sent + relays + list(z_sent.values()) + z_relays:
         cp.wait_send()
 
 
-def gather_tokens(z_bf, ids_t, group_n):
+def in_vmem(arr):
+    return pltpu.with_memory_space_constraint(arr, VMEM)
+
+
+def gather_tokens(z_bf, ids_t, group_n, n_loc):
     tok, d_model = z_bf.shape
     return pl.pallas_call(
-        gather_kernel,
-        out_shape=[jax.ShapeDtypeStruct((group_n, tok, d_model), BF16), jax.ShapeDtypeStruct((group_n, tok, 128), F32)],
+        functools.partial(gather_kernel, n_loc),
+        out_shape=[VMEM((group_n, tok, d_model), BF16), VMEM((group_n * tok, 128), F32), jax.ShapeDtypeStruct((8, 128), jnp.int32)],
         in_specs=[pl.BlockSpec(memory_space=VMEM)] * 2,
-        out_specs=[pl.BlockSpec(memory_space=VMEM)] * 2,
-        scratch_shapes=[VMEM((128, 128), F32), VMEM((tok, 128), F32), pltpu.SemaphoreType.DMA((7, 2)), pltpu.SemaphoreType.DMA((7, 2))],
-        compiler_params=pltpu.CompilerParams(collective_id=0, has_side_effects=True),
+        out_specs=[pl.BlockSpec(memory_space=VMEM)] * 3,
+        scratch_shapes=[VMEM((128, 128), F32), VMEM((8, 128), F32), VMEM((group_n, 8, 128), F32),
+                        pltpu.SemaphoreType.DMA((7, 2)), pltpu.SemaphoreType.DMA((7, 2))],
+        compiler_params=pltpu.CompilerParams(collective_id=0, has_side_effects=True, vmem_limit_bytes=16 * 1024 * 1024),
         name='gather_tokens',
-    )(z_bf, ids_t)
-
-
-def reduce_kernel(part_ref, hid_ref, out_ref, own, r1, s1, r2, s2, r3, send_sem, recv_sem):
+    )(in_vmem(z_bf), ids_t)
+
+
+def reduce_kernel(part_ref, hid_ref, out_ref, r1, s1, r2, s2, r3, send_sem, recv_sem):
     me, core, x, y, at = neighbours()
     twin, xn, yn = at(y, x, 1 - core), at(y, 1 - x, core), at(1 - y, x, core)
     entry_barrier([twin, xn, yn])
@@ -371,18 +417,17 @@
     half = d_model // 2
     return pl.pallas_call(
         reduce_kernel,
-        out_shape=jax.ShapeDtypeStruct((tok, d_model), BF16),
+        out_shape=VMEM((tok, d_model), BF16),
         in_specs=[pl.BlockSpec(memory_space=VMEM)] * 2,
         out_specs=pl.BlockSpec(memory_space=VMEM),
         scratch_shapes=[
-            VMEM((8, 128), F32),
             VMEM((4, tok, d_model), F32), VMEM((4, tok, d_model), F32),
             VMEM((2, 2, tok, half), F32), VMEM((2, tok, half), F32), VMEM((2, tok, half), F32),
             pltpu.SemaphoreType.DMA((10,)), pltpu.SemaphoreType.DMA((10,)),
         ],
-        compiler_params=pltpu.CompilerParams(collective_id=1, has_side_effects=True),
+        compiler_params=pltpu.CompilerParams(collective_id=1, has_side_effects=True, vmem_limit_bytes=16 * 1024 * 1024),
         name='reduce_outputs',
-    )(partial, hid_f32)
+    )(in_vmem(partial), in_vmem(hid_f32))
 
 
 ROWS = 128
@@ -390,36 +435,16 @@
 SLOTS = 6
 
 
-def expert_kernel(z_ref, ids_ref, rw_ref, b1_in, b2_in, w1_hbm, w2_hbm, out_ref,
-                  b1_ref, b2_ref, w1_buf, w2_buf, rank_s, gate_s, cnt_v, cnt_s, list_s, x_s, o_s, sem1, sem2, csem):
-    n_tok, d_model = z_ref.shape
+def expert_kernel(meta_sm, z_ref, cols_ref, rw_ref, b1_in, b2_in, w1_hbm, w2_hbm, out_ref,
+                  b1_ref, b2_ref, w1_buf, w2_buf, rank_s, gate_s, x_s, o_s, sem1, sem2):
+    n_tok, d_model = cols_ref.shape[0], z_ref.shape[2]
     n_loc = w1_hbm.shape[0]
     ff = w1_hbm.shape[2]
     fc = ff // SPLIT
-    n_blk = x_s.shape[0]
-    me = lax.axis_index('ep')
-    base = me * n_loc
-    lane = lax.broadcasted_iota(jnp.int32, (n_tok, 128), 1)
-    id0, id1 = ids_ref[:, 0:1].astype(jnp.int32), ids_ref[:, 1:2].astype(jnp.int32)
-    hit_loc = jnp.logical_or(id0 - base == lane, id1 - base == lane)
-    hit_loc = jnp.logical_and(hit_loc, lane < n_loc)
-    hit_t = hit_loc.astype(F32)
-    counts = jnp.sum(hit_t, axis=0, keepdims=True)
-    cnt_v[...] = jnp.broadcast_to(counts, cnt_v.shape).astype(jnp.int32)
-    cp = pltpu.make_async_copy(cnt_v, cnt_s, csem)
-    cp.start()
-    cp.wait()
-
-    def scan_body(e, n_act):
-        @pl.when(cnt_s[0, e] > 0)
-        def _():
-            list_s[n_act] = e
-        return n_act + jnp.where(cnt_s[0, e] > 0, 1, 0)
-    n_act = lax.fori_loop(0, n_loc, scan_body, 0)
-    n_step = n_act * SPLIT
+    n_step = meta_sm[2, 0] * SPLIT
 
     def copies(step, slot):
-        e = list_s[step // SPLIT]
+        e = meta_sm[1, step // SPLIT]
         f0 = pl.multiple_of((step % SPLIT) * fc, fc)
         return (pltpu.make_async_copy(w1_hbm.at[e, :, pl.ds(f0, fc)], w1_buf.at[slot], sem1.at[slot]),
                 pltpu.make_async_copy(w2_hbm.at[e, pl.ds(f0, fc), :], w2_buf.at[slot], sem2.at[slot]))
@@ -432,7 +457,9 @@
 
     b1_ref[...] = b1_in[...].astype(F32)
     b2_ref[...] = b2_in[...].astype(F32)
-    hit_bf = hit_t.astype(BF16)
+    z_all = z_ref[...].reshape(n_tok, d_model)
+    id0, id1, lane, hit_t = named_experts(cols_ref[...], lax.axis_index('ep') * n_loc, n_loc)
+    base = lax.axis_index('ep') * n_loc
     row_i = lax.broadcasted_iota(jnp.int32, (n_tok, n_tok), 0)
     col_i = lax.broadcasted_iota(jnp.int32, (n_tok, n_tok), 1)
     before = (row_i < col_i).astype(BF16)
@@ -440,22 +467,22 @@
     rank = jnp.dot(hit.astype(BF16), before, preferred_element_type=F32)
     rank_s[...] = jnp.where(hit > 0.5, rank, -1.0)
 
-    logits = jnp.dot(z_ref[...], rw_ref[...], preferred_element_type=F32)
+    logits = jnp.dot(z_all, rw_ref[...], preferred_element_type=F32)
     top = jnp.max(logits, axis=-1, keepdims=True)
     ex = jnp.exp(logits - top)
     probs = ex / jnp.sum(ex, axis=-1, keepdims=True)
-    p0 = jnp.sum(jnp.where(lane == id0, probs, 0.0), axis=-1, keepdims=True)
-    p1 = jnp.sum(jnp.where(lane == id1, probs, 0.0), axis=-1, keepdims=True)
+    p0 = jnp.sum(jnp.where(lane == id0 + base, probs, 0.0), axis=-1, keepdims=True)
+    p1 = jnp.sum(jnp.where(lane == id1 + base, probs, 0.0), axis=-1, keepdims=True)
     tot = p0 + p1
     g0, g1 = p0 / tot, p1 / tot
-    gate_s[...] = jnp.where(lane == id0 - base, g0, jnp.where(lane == id1 - base, g1, 0.0))
+    gate_s[...] = jnp.where(lane == id0, g0, jnp.where(lane == id1, g1, 0.0))
     out_ref[...] = jnp.zeros_like(out_ref)
 
     def step_body(step, carry):
         slot = step % SLOTS
-        e = list_s[step // SPLIT]
+        e = meta_sm[1, step // SPLIT]
         part = step % SPLIT
-        blocks = (cnt_s[0, e] + ROWS - 1) // ROWS
+        blocks = (meta_sm[0, e] + ROWS - 1) // ROWS
         slot_i = lax.broadcasted_iota(jnp.int32, (ROWS, n_tok), 0)
 
         def pick(j):
@@ -465,7 +492,7 @@
         @pl.when(part == 0)
         def _():
             def gather_body(j, c):
-                x_s[j] = jnp.dot(pick(j), z_ref[...], preferred_element_type=F32).astype(BF16)
+                x_s[j] = jnp.dot(pick(j), z_ref[...].reshape(n_tok, d_model), preferred_element_type=F32).astype(BF16)
                 o_s[j] = jnp.broadcast_to(b2_ref[pl.ds(e, 1), :], (ROWS, d_model))
                 return c
             lax.fori_loop(0, blocks, gather_body, 0)
@@ -493,7 +520,7 @@
 
             def scatter_body(j, c):
                 back = lax.dot_general(pick(j), o_s[j].astype(BF16), (((0,), (0,)), ((), ())), preferred_element_type=F32)
-                out_ref[...] += gate * back
+                out_ref[...] += (gate * back).reshape(out_ref.shape)
                 return c
             lax.fori_loop(0, blocks, scatter_body, 0)
         return carry
@@ -501,8 +528,9 @@
     lax.fori_loop(0, n_step, step_body, 0)
 
 
-def run_experts(z_all, ids_all, router_w, exp_w1, exp_b1, exp_w2, exp_b2):
-    n_tok, d_model = z_all.shape
+def run_experts(meta, z_all, cols, router_w, exp_w1, exp_b1, exp_w2, exp_b2):
+    group_n, tok, d_model = z_all.shape
+    n_tok = group_n * tok
     n_loc, _, ff = exp_w1.shape
     fc = ff // SPLIT
     n_blk = n_tok // ROWS
@@ -510,20 +538,19 @@
     hbm = pl.BlockSpec(memory_space=pl.ANY)
     return pl.pallas_call(
         expert_kernel,
-        out_shape=jax.ShapeDtypeStruct((n_tok, d_model), F32),
-        in_specs=[vm] * 5 + [hbm] * 2,
+        out_shape=VMEM((group_n, tok, d_model), F32),
+        in_specs=[pl.BlockSpec(memory_space=pltpu.SMEM)] + [vm] * 5 + [hbm] * 2,
         out_specs=vm,
         scratch_shapes=[
             VMEM((n_loc, ff), F32), VMEM((n_loc, d_model), F32),
             VMEM((SLOTS, d_model, fc), BF16), VMEM((SLOTS, fc, d_model), BF16),
             VMEM((128, n_tok), F32), VMEM((n_tok, 128), F32),
-            VMEM((8, 128), jnp.int32), pltpu.SMEM((8, 128), jnp.int32), pltpu.SMEM((n_loc,), jnp.int32),
             VMEM((n_blk, ROWS, d_model), BF16), VMEM((n_blk, ROWS, d_model), F32),
-            pltpu.SemaphoreType.DMA((SLOTS,)), pltpu.SemaphoreType.DMA((SLOTS,)), pltpu.SemaphoreType.DMA,
+            pltpu.SemaphoreType.DMA((SLOTS,)), pltpu.SemaphoreType.DMA((SLOTS,)),
         ],
-        compiler_params=pltpu.CompilerParams(vmem_limit_bytes=60 * 1024 * 1024),
+        compiler_params=pltpu.CompilerParams(vmem_limit_bytes=48 * 1024 * 1024),
         name='run_experts',
-    )(z_all, ids_all, router_w, exp_b1, exp_b2, exp_w1, exp_w2)
+    )(meta, in_vmem(z_all), in_vmem(cols), router_w, exp_b1, exp_b2, exp_w1, exp_w2)
 
 
 def solution(mesh):
@@ -531,10 +558,9 @@
 
     def local_step(hidden, self_pos, src_len, cache_a, cross_a, cache_b, cross_b, route_ids, ln_gain, ln_shift, attn_w, attn_b, ffn_w1, ffn_b1, ffn_w2, ffn_b2, router_w, exp_w1, exp_b1, exp_w2, exp_b2):
         hid_f32, z_bf, cache_a_new, cache_b_new = dense_layers(hidden, self_pos, src_len, cache_a, cross_a, cache_b, cross_b, ln_gain, ln_shift, attn_w, attn_b, ffn_w1, ffn_b1, ffn_w2, ffn_b2)
-        tok, d_model = z_bf.shape
-        z_all, ids_all = gather_tokens(z_bf, route_ids.T, group_n)
-        partial = run_experts(z_all.reshape(-1, d_model), ids_all.reshape(-1, 128), router_w, exp_w1, exp_b1, exp_w2, exp_b2)
-        out = reduce_outputs(partial.reshape(group_n, tok, d_model), hid_f32)
+        z_all, cols, meta = gather_tokens(z_bf, route_ids.T, group_n, exp_w1.shape[0])
+        partial = run_experts(meta, z_all, cols, router_w, exp_w1, exp_b1, exp_w2, exp_b2)
+        out = reduce_outputs(partial, hid_f32)
         return out, cache_a_new, cache_b_new
 
     tok_spec = P(('dp', 'ep'))

time: 94.8 us -> 74.5 us (0.79)
  Pallas kernels: 90.8 us -> 73.3 us
  local copies, waits for them, and re-layouts: 2.89 us -> 0.66 us
    pallas_call x4, Pallas kernels: 90.8 us -> 73.3 us  [the longest x1 33.7 us: dense_layers(): pl.pallas_call(dense_kernel, out_shape=[VMEM((tok, d_model), F32), VMEM((...]
    reshape x1 -> x0, local copies, waits for them, and re-layouts: 1.35 us -> none  [dense_layers(): self_pos.reshape(-1, 1)]
where the time goes in v2:
time: 74.5 us; the launch traced here: 74.6 us
  Pallas kernels  73.3 us (98%)
    pallas_call x1, Pallas kernels, dense_layers(): pl.pallas_call(dense_kernel, out_shape=[VMEM((tok, d_model), F32), VMEM((...  33.7 us
    pallas_call x1, Pallas kernels, run_experts(): pl.pallas_call(expert_kernel, out_shape=VMEM((group_n, tok, d_model), F32...  15.6 us
    pallas_call x1, Pallas kernels, reduce_outputs(): pl.pallas_call(reduce_kernel, out_shape=VMEM((tok, d_model), BF16), in_sp...  12.7 us
    pallas_call x1, Pallas kernels, gather_tokens(): pl.pallas_call(functools.partial(gather_kernel, n_loc), out_shape=[VMEM((...  11.2 us

profile of v2, /device:TPU:0, one launch (start us, length us, event | category | flops | bytes accessed | tf_op | source)
XLA Modules:
  0.0 74.6 jit_solution(1201359816633005554)
XLA Ops:
  0.6 0.0 copy-start.3
  0.6 0.0 copy-start
  0.7 0.0 copy-start.1
  0.7 0.0 copy-start.2
  0.7 33.7 %dense_layers.1 = (f32[64,768]{1,0:T(8,128)S(1)}, bf16[64,768]{1,0:T(8,128)(2,1)S(1)}, bf16[2,64,12,16,64]{4,3,2,1,0:T(8,128)(2,1)}, bf16[2,64,12,16,64]{4,3,2,1,0:T(8,128)(2,1)}) custom-call(s32[64]{0:T(128)} %pos_sm.1, s32[64]{0:T(128)} %len_sm.1, bf16[64,768]{1,0:T(8,128)(2,1)} %hid_ref.1, f32[3,2,768]{2,1,0:T(2,128)} %bitcast.15, f32[3,2,768]{2,1,0:T(2,128)} %bitcast.16, ...), custom_call_target="tpu_custom_call" | custom-call | tf_op jit(solution)/shard_map/dense_layers/pallas_call | solution.py:242
  34.3 0.0 copy-done.3
  34.3 11.2 %gather_tokens.1 = (bf16[8,64,768]{2,1,0:T(8,128)(2,1)S(1)}, f32[512,128]{1,0:T(8,128)S(1)}, s32[8,128]{1,0:T(8,128)S(1)}) custom-call(bf16[64,768]{1,0:T(8,128)(2,1)S(1)} %get-tuple-element.10.z_ref, s32[2,64]{1,0:T(2,128)S(1)} %bitcast.10), custom_call_target="tpu_custom_call" | custom-call | tf_op jit(solution)/shard_map/gather_tokens/pallas_call | solution.py:357
  45.6 0.0 copy-done
  45.6 0.0 copy-done.1
  45.6 0.0 copy-done.2
  45.6 15.6 %run_experts.1.part_ref = f32[8,64,768]{2,1,0:T(8,128)S(1)} custom-call(s32[8,128]{1,0:T(8,128)S(1)} %get-tuple-element.11.meta_sm, bf16[8,64,768]{2,1,0:T(8,128)(2,1)S(1)} %get-tuple-element.12.z_ref, f32[512,128]{1,0:T(8,128)S(1)} %get-tuple-element.13.cols_ref, bf16[768,128]{1,0:T(8,128)(2,1)S(1)} %copy-done, bf16[16,3072]{1,0:T(8,128)(2,1)S(1)} %copy-done.1, ...), custom_call_target="tpu_custom_call" | custom-call | tf_op jit(solution)/shard_map/run_experts/pallas_call | solution.py:539
  61.2 12.7 %reduce_outputs.1 = bf16[64,768]{1,0:T(8,128)(2,1)S(1)} custom-call(f32[8,64,768]{2,1,0:T(8,128)S(1)} %run_experts.1.part_ref, f32[64,768]{1,0:T(8,128)S(1)} %get-tuple-element.14.hid_ref), custom_call_target="tpu_custom_call" | custom-call | tf_op jit(solution)/shard_map/reduce_outputs/pallas_call | solution.py:418
  74.0 0.6 copy.25
Async XLA Ops:
  0.6 33.7 %copy-start.3 = (s32[64,2]{0,1:T(2,128)S(1)}, s32[64,2]{0,1:T(2,128)}, u32[]{:S(2)}) copy-start(s32[64,2]{0,1:T(2,128)} %param.28) | copy-start | bytes 1540
  0.6 45.0 %copy-start = (bf16[768,128]{1,0:T(8,128)(2,1)S(1)}, bf16[768,128]{1,0:T(8,128)(2,1)}, u32[]{:S(2)}) copy-start(bf16[768,128]{1,0:T(8,128)(2,1)} %rw_ref.1) | copy-start | bytes 589828
  0.7 45.0 %copy-start.1 = (bf16[16,3072]{1,0:T(8,128)(2,1)S(1)}, bf16[16,3072]{1,0:T(8,128)(2,1)}, u32[]{:S(2)}) copy-start(bf16[16,3072]{1,0:T(8,128)(2,1)} %b1_in.1) | copy-start | bytes 294916
  0.7 45.0 %copy-start.2 = (bf16[16,768]{1,0:T(8,128)(2,1)S(1)}, bf16[16,768]{1,0:T(8,128)(2,1)}, u32[]{:S(2)}) copy-start(bf16[16,768]{1,0:T(8,128)(2,1)} %b2_in.1) | copy-start | bytes 73732

commit v3 on v2

--- a/solution.py
+++ b/solution.py
@@ -14,10 +14,10 @@
 
 
 CROSS_GROUP = 16
-CROSS_UNIT = 1
 SELF_GROUP = 16
-SELF_UNIT = 2
+SELF_UNIT = 4
 HEAD_PAD = 16
+PAIR_PAD = 8
 
 
 def norm_rows(x_val, gain_vec, shift_vec):
@@ -87,11 +87,15 @@
         return lax.fori_loop(cross_rows(b) // 16, src // 16, zero_part, c)
     lax.fori_loop(0, tok, zero_tail, 0)
 
+    n_pairs = n_heads // 2
+    wide = 2 * head_dim
+
     def build_mask(ref, length):
         row = lax.broadcasted_iota(jnp.int32, ref.shape, 0)
         lane = lax.broadcasted_iota(jnp.int32, ref.shape, 1)
-        seq, head = lane // (n_heads * length), (lane // length) % n_heads
-        ref[...] = jnp.where(seq * HEAD_PAD + head == row, lane % length, 1 << 20)
+        seq, pair = lane // (n_pairs * length), (lane // length) % n_pairs
+        same = jnp.logical_and(seq == row // HEAD_PAD, pair == (row % HEAD_PAD) // 2)
+        ref[...] = jnp.where(same, lane % length, 1 << 20)
     build_mask(self_mask, self_len)
     build_mask(cross_mask, src)
 
@@ -100,15 +104,25 @@
         return c
     lax.fori_loop(0, tok, fill_limit, 0)
 
+    even_half = lax.broadcasted_iota(jnp.int32, (tok, wide), 1) < head_dim
+
+    def pairs_of(val):
+        val = val.astype(BF16).astype(F32)
+        return [val[:, j * wide:(j + 1) * wide] for j in range(n_pairs)]
+
     def to_heads(ref, val):
-        val = val.astype(BF16).astype(F32)
-        for h in range(n_heads):
-            ref[pl.ds(h, tok, stride=HEAD_PAD), :] = val[:, h * head_dim:(h + 1) * head_dim]
+        for j, two in enumerate(pairs_of(val)):
+            ref[pl.ds(2 * j, tok, stride=HEAD_PAD), :] = jnp.where(even_half, two, 0.0)
+            ref[pl.ds(2 * j + 1, tok, stride=HEAD_PAD), :] = jnp.where(even_half, 0.0, two)
+
+    def to_pairs(ref, val):
+        for j, two in enumerate(pairs_of(val)):
+            ref[pl.ds(j, tok, stride=PAIR_PAD), :] = two
 
     def from_heads(ref):
-        for h in range(0, n_heads, 2):
-            two = [ref[pl.ds(h + k, tok, stride=HEAD_PAD), :] for k in range(2)]
-            cat_s[:, h * head_dim:(h + 2) * head_dim] = jnp.concatenate(two, axis=1).astype(BF16)
+        for j in range(n_pairs):
+            two = jnp.where(even_half, ref[pl.ds(2 * j, tok, stride=HEAD_PAD), :], ref[pl.ds(2 * j + 1, tok, stride=HEAD_PAD), :])
+            cat_s[:, j * wide:(j + 1) * wide] = two.astype(BF16)
         return cat_s[...]
 
     def softmax_rows(scores, mask, limit):
@@ -120,13 +134,6 @@
     def scores_of(q, keys):
         return lax.dot_general(q, keys, (((1,), (1,)), ((), ())), preferred_element_type=F32)
 
-    def block_diag(blocks):
-        rows = []
-        for k, blk in enumerate(blocks):
-            pad = jnp.zeros_like(blk)
-            rows.append(jnp.concatenate([blk if j == k else pad for j in range(len(blocks))], axis=1))
-        return jnp.concatenate(rows, axis=0)
-
     def proj(layer, i, x_bf):
         weight_copy(layer * 6 + i).wait()
         bias = ab_ref[i].astype(F32)[layer:layer + 1, :]
@@ -135,9 +142,9 @@
     def self_layer(layer, h, cache, cache_out):
         x = norm_rows(h, gain_ref[0, layer:layer + 1, :], shift_ref[0, layer:layer + 1, :])
         to_heads(q_s, proj(layer, 0, x))
-        to_heads(k_s, proj(layer, 1, x))
-        to_heads(v_s, proj(layer, 2, x))
-        row_i = lax.broadcasted_iota(jnp.int32, (self_len, head_dim), 0)
+        to_pairs(k_s, proj(layer, 1, x))
+        to_pairs(v_s, proj(layer, 2, x))
+        row_i = lax.broadcasted_iota(jnp.int32, (self_len, wide), 0)
         row_b = row_i.astype(F32).astype(BF16)
 
         def body(g, c):
@@ -149,26 +156,23 @@
                 for u in range(SELF_GROUP):
                     b = first + u
                     hit = row_b == jnp.full(row_b.shape, pos_sm[b], jnp.int32).astype(F32).astype(BF16)
-                    for hd in range(n_heads):
-                        row = new[pl.ds(b * HEAD_PAD + hd, self_len, stride=0), :]
-                        tile = jnp.where(hit, row.astype(BF16), self_buf[which, b, hd])
-                        self_buf[which, b, hd] = tile
-                        tiles.append(tile)
+                    for j in range(n_pairs):
+                        row = new[pl.ds(b * PAIR_PAD + j, self_len, stride=0), :].astype(BF16)
+                        two = jnp.concatenate([self_buf[which, b, 2 * j], self_buf[which, b, 2 * j + 1]], axis=1)
+                        two = jnp.where(hit, row, two)
+                        self_buf[which, b, 2 * j] = two[:, :head_dim]
+                        self_buf[which, b, 2 * j + 1] = two[:, head_dim:]
+                        tiles.append(two)
                 sides.append(tiles)
             n = SELF_UNIT
             parts = range(0, SELF_GROUP, n)
-            wide = n * n_heads * self_len
-            stack = lambda tiles, p: jnp.concatenate(tiles[p * n_heads:(p + n) * n_heads], axis=0)
+            stack = lambda tiles, p: jnp.concatenate(tiles[p * n_pairs:(p + n) * n_pairs], axis=0)
             scores = [scores_of(q_s[head_rows(first + p, n), :].astype(BF16), stack(sides[0], p)) for p in parts]
             probs = []
             for p, sc in zip(parts, scores):
-                two = 2 * n_heads * self_len
-                blocks = []
-                for k in range(n // 2):
-                    lim = lim_s[head_rows(first + p + 2 * k, 2), :]
-                    lim = jnp.concatenate([lim] * (two // 128), axis=1)
-                    blocks.append(softmax_rows(sc[k * 2 * HEAD_PAD:(k + 1) * 2 * HEAD_PAD, k * two:(k + 1) * two], self_mask[...], lim))
-                probs.append(block_diag(blocks))
+                lim = lim_s[head_rows(first + p, n), :]
+                lim = jnp.concatenate([lim] * (sc.shape[1] // 128), axis=1)
+                probs.append(softmax_rows(sc, self_mask[...], lim))
             for p, pr in zip(parts, probs):
                 ctx_s[head_rows(first + p, n), :] = jnp.dot(pr, stack(sides[1], p), preferred_element_type=F32)
             self_out(cache_out, g).start()
@@ -185,16 +189,14 @@
             first = g * CROSS_GROUP
             for u in range(CROSS_GROUP):
                 cross_copy(cross, first + u).wait()
-            n = CROSS_UNIT
-            parts = [first + p for p in range(0, CROSS_GROUP, n)]
-            wide = n_heads * src
-            scores = [scores_of(q_s[head_rows(at, n), :].astype(BF16), cross_buf[pl.ds(at, n), 0].reshape(n * wide, head_dim)) for at in parts]
-            probs = []
-            for at, sc in zip(parts, scores):
-                probs.append(block_diag([softmax_rows(sc[u * HEAD_PAD:(u + 1) * HEAD_PAD, u * wide:(u + 1) * wide], cross_mask[...], len_sm[at + u]) for u in range(n)]))
-            for at, pr in zip(parts, probs):
-                vals = cross_buf[pl.ds(at, n), 1].reshape(n * wide, head_dim)
-                ctx_s[head_rows(at, n), :] = jnp.dot(pr, vals, preferred_element_type=F32)
+            def side(b, which):
+                return jnp.concatenate([jnp.concatenate([cross_buf[b, which, 2 * j], cross_buf[b, which, 2 * j + 1]], axis=1) for j in range(n_pairs)], axis=0)
+
+            group = [first + u for u in range(CROSS_GROUP)]
+            scores = [scores_of(q_s[head_rows(b, 1), :].astype(BF16), side(b, 0)) for b in group]
+            probs = [softmax_rows(sc, cross_mask[...], len_sm[b]) for b, sc in zip(group, scores)]
+            for b, pr in zip(group, probs):
+                ctx_s[head_rows(b, 1), :] = jnp.dot(pr, side(b, 1), preferred_element_type=F32)
             if after is not None:
                 for u in range(CROSS_GROUP):
                     cross_copy(after, first + u).start()
@@ -238,7 +240,9 @@
     hbm = pl.BlockSpec(memory_space=pl.ANY)
     cache_t = jax.ShapeDtypeStruct((2, tok, n_heads, self_len, head_dim), BF16)
     n_self = tok // SELF_GROUP
-    heads = VMEM((tok * HEAD_PAD, head_dim), F32)
+    heads = VMEM((tok * HEAD_PAD, 2 * head_dim), F32)
+    pairs = VMEM((tok * PAIR_PAD, 2 * head_dim), F32)
+    half = n_heads // 2
     hid, z, out_a, out_b = pl.pallas_call(
         dense_kernel,
         out_shape=[VMEM((tok, d_model), F32), VMEM((tok, d_model), BF16), cache_t, cache_t],
@@ -247,8 +251,8 @@
         scratch_shapes=[
             VMEM((12, d_model, d_model), BF16), VMEM((d_model, ff), BF16), VMEM((ff, d_model), BF16),
             VMEM((2, tok, n_heads, self_len, head_dim), BF16), VMEM((tok, 2, n_heads, src, head_dim), BF16),
-            heads, heads, heads, heads, VMEM((tok, d_model), BF16), VMEM((tok * HEAD_PAD, 128), jnp.int32),
-            VMEM((2 * HEAD_PAD, 2 * n_heads * self_len), jnp.int32), VMEM((HEAD_PAD, n_heads * src), jnp.int32),
+            heads, pairs, pairs, heads, VMEM((tok, d_model), BF16), VMEM((tok * HEAD_PAD, 128), jnp.int32),
+            VMEM((SELF_UNIT * HEAD_PAD, SELF_UNIT * half * self_len), jnp.int32), VMEM((HEAD_PAD, half * src), jnp.int32),
             pltpu.SemaphoreType.DMA((12,)), pltpu.SemaphoreType.DMA((2,)), pltpu.SemaphoreType.DMA((n_self,)),
             pltpu.SemaphoreType.DMA((n_self,)), pltpu.SemaphoreType.DMA((tok,)),
         ],

time: 74.5 us -> 139 us (1.87)
  Pallas kernels: 73.3 us -> 138 us
    pallas_call x1, Pallas kernels: 33.7 us -> 97.1 us  [dense_layers(): pl.pallas_call(dense_kernel, out_shape=[VMEM((tok, d_model), F32), VMEM((...]
where the time goes in v3:
time: 139 us
  Pallas kernels  138 us (99%)
    pallas_call x1, Pallas kernels, dense_layers(): pl.pallas_call(dense_kernel, out_shape=[VMEM((tok, d_model), F32), VMEM((...  97.1 us
    pallas_call x1, Pallas kernels, run_experts(): pl.pallas_call(expert_kernel, out_shape=VMEM((group_n, tok, d_model), F32...  15.6 us
    pallas_call x1, Pallas kernels, reduce_outputs(): pl.pallas_call(reduce_kernel, out_shape=VMEM((tok, d_model), BF16), in_sp...  13.8 us
    pallas_call x1, Pallas kernels, gather_tokens(): pl.pallas_call(functools.partial(gather_kernel, n_loc), out_shape=[VMEM((...  11.3 us

profile of v3, /device:TPU:0, one launch (start us, length us, event | category | flops | bytes accessed | tf_op | source)
XLA Modules:
  0.0 139.2 jit_solution(5194026232573468435)
XLA Ops:
  0.6 0.0 copy-start.3
  0.6 0.0 copy-start
  0.7 0.0 copy-start.1
  0.7 0.0 copy-start.2
  0.7 97.1 %dense_layers.1 = (f32[64,768]{1,0:T(8,128)S(1)}, bf16[64,768]{1,0:T(8,128)(2,1)S(1)}, bf16[2,64,12,16,64]{4,3,2,1,0:T(8,128)(2,1)}, bf16[2,64,12,16,64]{4,3,2,1,0:T(8,128)(2,1)}) custom-call(s32[64]{0:T(128)} %pos_sm.1, s32[64]{0:T(128)} %len_sm.1, bf16[64,768]{1,0:T(8,128)(2,1)} %hid_ref.1, f32[3,2,768]{2,1,0:T(2,128)} %bitcast.15, f32[3,2,768]{2,1,0:T(2,128)} %bitcast.16, ...), custom_call_target="tpu_custom_call" | custom-call | tf_op jit(solution)/shard_map/dense_layers/pallas_call | solution.py:246
  97.8 0.0 copy-done.3
  97.8 11.3 %gather_tokens.1 = (bf16[8,64,768]{2,1,0:T(8,128)(2,1)S(1)}, f32[512,128]{1,0:T(8,128)S(1)}, s32[8,128]{1,0:T(8,128)S(1)}) custom-call(bf16[64,768]{1,0:T(8,128)(2,1)S(1)} %get-tuple-element.10.z_ref, s32[2,64]{1,0:T(2,128)S(1)} %bitcast.10), custom_call_target="tpu_custom_call" | custom-call | tf_op jit(solution)/shard_map/gather_tokens/pallas_call | solution.py:361
  109.1 0.0 copy-done
  109.1 0.0 copy-done.1
  109.1 0.0 copy-done.2
  109.1 15.6 %run_experts.1.part_ref = f32[8,64,768]{2,1,0:T(8,128)S(1)} custom-call(s32[8,128]{1,0:T(8,128)S(1)} %get-tuple-element.11.meta_sm, bf16[8,64,768]{2,1,0:T(8,128)(2,1)S(1)} %get-tuple-element.12.z_ref, f32[512,128]{1,0:T(8,128)S(1)} %get-tuple-element.13.cols_ref, bf16[768,128]{1,0:T(8,128)(2,1)S(1)} %copy-done, bf16[16,3072]{1,0:T(8,128)(2,1)S(1)} %copy-done.1, ...), custom_call_target="tpu_custom_call" | custom-call | tf_op jit(solution)/shard_map/run_experts/pallas_call | solution.py:543
  124.8 13.8 %reduce_outputs.1 = bf16[64,768]{1,0:T(8,128)(2,1)S(1)} custom-call(f32[8,64,768]{2,1,0:T(8,128)S(1)} %run_experts.1.part_ref, f32[64,768]{1,0:T(8,128)S(1)} %get-tuple-element.14.hid_ref), custom_call_target="tpu_custom_call" | custom-call | tf_op jit(solution)/shard_map/reduce_outputs/pallas_call | solution.py:422
  138.5 0.6 copy.25
Async XLA Ops:
  0.6 97.2 %copy-start.3 = (s32[64,2]{0,1:T(2,128)S(1)}, s32[64,2]{0,1:T(2,128)}, u32[]{:S(2)}) copy-start(s32[64,2]{0,1:T(2,128)} %param.28) | copy-start | bytes 1540
  0.6 108.5 %copy-start = (bf16[768,128]{1,0:T(8,128)(2,1)S(1)}, bf16[768,128]{1,0:T(8,128)(2,1)}, u32[]{:S(2)}) copy-start(bf16[768,128]{1,0:T(8,128)(2,1)} %rw_ref.1) | copy-start | bytes 589828
  0.7 108.5 %copy-start.1 = (bf16[16,3072]{1,0:T(8,128)(2,1)S(1)}, bf16[16,3072]{1,0:T(8,128)(2,1)}, u32[]{:S(2)}) copy-start(bf16[16,3072]{1,0:T(8,128)(2,1)} %b1_in.1) | copy-start | bytes 294916
  0.7 108.5 %copy-start.2 = (bf16[16,768]{1,0:T(8,128)(2,1)S(1)}, bf16[16,768]{1,0:T(8,128)(2,1)}, u32[]{:S(2)}) copy-start(bf16[16,768]{1,0:T(8,128)(2,1)} %b2_in.1) | copy-start | bytes 73732

commit v4 on v2

--- a/solution.py
+++ b/solution.py
@@ -14,7 +14,7 @@
 
 
 CROSS_GROUP = 16
-CROSS_UNIT = 1
+ROW_STEP = 16
 SELF_GROUP = 16
 SELF_UNIT = 2
 HEAD_PAD = 16
@@ -30,13 +30,15 @@
 def dense_kernel(pos_sm, len_sm, hid_ref, gain_ref, shift_ref, ab_ref, fb1_ref, fb2_ref,
                  cache_a, cross_a, cache_b, cross_b, aw_hbm, w1_hbm, w2_hbm,
                  hid_out, z_out, cache_a_out, cache_b_out,
-                 w_buf, f1_buf, f2_buf, self_buf, cross_buf, q_s, k_s, v_s, ctx_s, cat_s, lim_s, self_mask, cross_mask,
+                 w_buf, f1_buf, f2_buf, self_buf, cross_buf, q_s, k_s, v_s, ctx_s, cat_s, lim_s, self_mask, mask_1, mask_2, mask_3, mask_4, order_sm, place_sm,
                  w_sem, f_sem, in_sem, out_sem, cross_sem):
     tok, d_model = hid_ref.shape
     n_heads, self_len, head_dim = self_buf.shape[2:]
     src = cross_buf.shape[3]
     ff = f1_buf.shape[1]
     scale = head_dim ** -0.5
+    cross_masks = (mask_1, mask_2, mask_3, mask_4)
+    n_class = len(cross_masks)
     n_self = tok // SELF_GROUP
 
     def head_rows(b, n):
@@ -58,6 +60,31 @@
 
     def cross_rows(b):
         return pl.multiple_of(((len_sm[b] + 15) // 16) * 16, 16)
+
+    def length_class(b):
+        return (len_sm[b] + (ROW_STEP - 1)) // ROW_STEP - 1
+
+    def sort_by_length():
+        for k in range(n_class):
+            place_sm[k] = 0
+
+        def count(b, c):
+            k = length_class(b)
+            place_sm[k] = place_sm[k] + 1
+            return c
+        lax.fori_loop(0, tok, count, 0)
+        start = 0
+        for k in range(n_class):
+            here = place_sm[k]
+            place_sm[k] = start
+            start = start + here
+
+        def put(b, c):
+            k = length_class(b)
+            order_sm[place_sm[k]] = b
+            place_sm[k] = place_sm[k] + 1
+            return c
+        lax.fori_loop(0, tok, put, 0)
 
     def cross_copy(cross, b):
         rows = pl.ds(0, cross_rows(b))
@@ -70,8 +97,10 @@
     weight_copy(3).start()
     weight_copy(4).start()
 
-    def first_cross(b, c):
-        cross_copy(cross_a, b).start()
+    sort_by_length()
+
+    def first_cross(i, c):
+        cross_copy(cross_a, order_sm[i]).start()
         return c
     lax.fori_loop(0, tok, first_cross, 0)
     weight_copy(5).start()
@@ -93,7 +122,8 @@
         seq, head = lane // (n_heads * length), (lane // length) % n_heads
         ref[...] = jnp.where(seq * HEAD_PAD + head == row, lane % length, 1 << 20)
     build_mask(self_mask, self_len)
-    build_mask(cross_mask, src)
+    for mask in cross_masks:
+        build_mask(mask, mask.shape[1] // n_heads)
 
     def fill_limit(b, c):
         lim_s[head_rows(b, 1), :] = jnp.full((HEAD_PAD, 128), pos_sm[b] + 1, jnp.int32)
@@ -182,22 +212,22 @@
         to_heads(q_s, proj(layer, 4, x))
 
         def body(g, c):
-            first = g * CROSS_GROUP
-            for u in range(CROSS_GROUP):
-                cross_copy(cross, first + u).wait()
-            n = CROSS_UNIT
-            parts = [first + p for p in range(0, CROSS_GROUP, n)]
-            wide = n_heads * src
-            scores = [scores_of(q_s[head_rows(at, n), :].astype(BF16), cross_buf[pl.ds(at, n), 0].reshape(n * wide, head_dim)) for at in parts]
-            probs = []
-            for at, sc in zip(parts, scores):
-                probs.append(block_diag([softmax_rows(sc[u * HEAD_PAD:(u + 1) * HEAD_PAD, u * wide:(u + 1) * wide], cross_mask[...], len_sm[at + u]) for u in range(n)]))
-            for at, pr in zip(parts, probs):
-                vals = cross_buf[pl.ds(at, n), 1].reshape(n * wide, head_dim)
-                ctx_s[head_rows(at, n), :] = jnp.dot(pr, vals, preferred_element_type=F32)
+            group = [order_sm[g * CROSS_GROUP + u] for u in range(CROSS_GROUP)]
+            longest = length_class(group[-1])
+            for b in group:
+                cross_copy(cross, b).wait()
+            for k, mask in enumerate(cross_masks):
+                @pl.when(longest == k)
+                def _():
+                    rows = mask.shape[1] // n_heads
+                    side = lambda b, which: cross_buf[b, which, :, 0:rows, :].reshape(n_heads * rows, head_dim)
+                    scores = [scores_of(q_s[head_rows(b, 1), :].astype(BF16), side(b, 0)) for b in group]
+                    probs = [softmax_rows(sc, mask[...], len_sm[b]) for b, sc in zip(group, scores)]
+                    for b, pr in zip(group, probs):
+                        ctx_s[head_rows(b, 1), :] = jnp.dot(pr, side(b, 1), preferred_element_type=F32)
             if after is not None:
-                for u in range(CROSS_GROUP):
-                    cross_copy(after, first + u).start()
+                for b in group:
+                    cross_copy(after, b).start()
             return c
         lax.fori_loop(0, tok // CROSS_GROUP, body, 0)
         ctx = from_heads(ctx_s)
@@ -248,7 +278,8 @@
             VMEM((12, d_model, d_model), BF16), VMEM((d_model, ff), BF16), VMEM((ff, d_model), BF16),
             VMEM((2, tok, n_heads, self_len, head_dim), BF16), VMEM((tok, 2, n_heads, src, head_dim), BF16),
             heads, heads, heads, heads, VMEM((tok, d_model), BF16), VMEM((tok * HEAD_PAD, 128), jnp.int32),
-            VMEM((2 * HEAD_PAD, 2 * n_heads * self_len), jnp.int32), VMEM((HEAD_PAD, n_heads * src), jnp.int32),
+            VMEM((2 * HEAD_PAD, 2 * n_heads * self_len), jnp.int32), ] + [VMEM((HEAD_PAD, n_heads * rows), jnp.int32) for rows in range(ROW_STEP, src + 1, ROW_STEP)] + [
+            pltpu.SMEM((tok,), jnp.int32), pltpu.SMEM((8,), jnp.int32),
             pltpu.SemaphoreType.DMA((12,)), pltpu.SemaphoreType.DMA((2,)), pltpu.SemaphoreType.DMA((n_self,)),
             pltpu.SemaphoreType.DMA((n_self,)), pltpu.SemaphoreType.DMA((tok,)),
         ],

time: 74.5 us -> 76.9 us (1.032)
  Pallas kernels: 73.3 us -> 75.6 us
    pallas_call x1, Pallas kernels: 12.7 us -> 13.8 us  [reduce_outputs(): pl.pallas_call(reduce_kernel, out_shape=VMEM((tok, d_model), BF16), in_sp...]
where the time goes in v4:
time: 76.9 us; the launch traced here: 77 us
  Pallas kernels  75.6 us (98%)
    pallas_call x1, Pallas kernels, dense_layers(): pl.pallas_call(dense_kernel, out_shape=[VMEM((tok, d_model), F32), VMEM((...  34.2 us
    pallas_call x1, Pallas kernels, run_experts(): pl.pallas_call(expert_kernel, out_shape=VMEM((group_n, tok, d_model), F32...  15.6 us
    pallas_call x1, Pallas kernels, reduce_outputs(): pl.pallas_call(reduce_kernel, out_shape=VMEM((tok, d_model), BF16), in_sp...  13.8 us
    pallas_call x1, Pallas kernels, gather_tokens(): pl.pallas_call(functools.partial(gather_kernel, n_loc), out_shape=[VMEM((...  12 us

profile of v4, /device:TPU:0, one launch (start us, length us, event | category | flops | bytes accessed | tf_op | source)
XLA Modules:
  0.0 77.0 jit_solution(1556608295446317915)
XLA Ops:
  0.6 0.0 copy-start.3
  0.6 0.0 copy-start
  0.7 0.0 copy-start.1
  0.7 0.0 copy-start.2
  0.7 34.2 %dense_layers.1 = (f32[64,768]{1,0:T(8,128)S(1)}, bf16[64,768]{1,0:T(8,128)(2,1)S(1)}, bf16[2,64,12,16,64]{4,3,2,1,0:T(8,128)(2,1)}, bf16[2,64,12,16,64]{4,3,2,1,0:T(8,128)(2,1)}) custom-call(s32[64]{0:T(128)} %pos_sm.1, s32[64]{0:T(128)} %len_sm.1, bf16[64,768]{1,0:T(8,128)(2,1)} %hid_ref.1, f32[3,2,768]{2,1,0:T(2,128)} %bitcast.15, f32[3,2,768]{2,1,0:T(2,128)} %bitcast.16, ...), custom_call_target="tpu_custom_call" | custom-call | tf_op jit(solution)/shard_map/dense_layers/pallas_call | solution.py:272
  34.8 0.0 copy-done.3
  34.9 12.0 %gather_tokens.1 = (bf16[8,64,768]{2,1,0:T(8,128)(2,1)S(1)}, f32[512,128]{1,0:T(8,128)S(1)}, s32[8,128]{1,0:T(8,128)S(1)}) custom-call(bf16[64,768]{1,0:T(8,128)(2,1)S(1)} %get-tuple-element.10.z_ref, s32[2,64]{1,0:T(2,128)S(1)} %bitcast.10), custom_call_target="tpu_custom_call" | custom-call | tf_op jit(solution)/shard_map/gather_tokens/pallas_call | solution.py:388
  46.8 0.0 copy-done
  46.9 0.0 copy-done.1
  46.9 0.0 copy-done.2
  46.9 15.6 %run_experts.1.part_ref = f32[8,64,768]{2,1,0:T(8,128)S(1)} custom-call(s32[8,128]{1,0:T(8,128)S(1)} %get-tuple-element.11.meta_sm, bf16[8,64,768]{2,1,0:T(8,128)(2,1)S(1)} %get-tuple-element.12.z_ref, f32[512,128]{1,0:T(8,128)S(1)} %get-tuple-element.13.cols_ref, bf16[768,128]{1,0:T(8,128)(2,1)S(1)} %copy-done, bf16[16,3072]{1,0:T(8,128)(2,1)S(1)} %copy-done.1, ...), custom_call_target="tpu_custom_call" | custom-call | tf_op jit(solution)/shard_map/run_experts/pallas_call | solution.py:570
  62.5 13.8 %reduce_outputs.1 = bf16[64,768]{1,0:T(8,128)(2,1)S(1)} custom-call(f32[8,64,768]{2,1,0:T(8,128)S(1)} %run_experts.1.part_ref, f32[64,768]{1,0:T(8,128)S(1)} %get-tuple-element.14.hid_ref), custom_call_target="tpu_custom_call" | custom-call | tf_op jit(solution)/shard_map/reduce_outputs/pallas_call | solution.py:449
  76.3 0.6 copy.25
Async XLA Ops:
  0.6 34.2 %copy-start.3 = (s32[64,2]{0,1:T(2,128)S(1)}, s32[64,2]{0,1:T(2,128)}, u32[]{:S(2)}) copy-start(s32[64,2]{0,1:T(2,128)} %param.28) | copy-start | bytes 1540
  0.6 46.2 %copy-start = (bf16[768,128]{1,0:T(8,128)(2,1)S(1)}, bf16[768,128]{1,0:T(8,128)(2,1)}, u32[]{:S(2)}) copy-start(bf16[768,128]{1,0:T(8,128)(2,1)} %rw_ref.1) | copy-start | bytes 589828
  0.7 46.2 %copy-start.1 = (bf16[16,3072]{1,0:T(8,128)(2,1)S(1)}, bf16[16,3072]{1,0:T(8,128)(2,1)}, u32[]{:S(2)}) copy-start(bf16[16,3072]{1,0:T(8,128)(2,1)} %b1_in.1) | copy-start | bytes 294916
  0.7 46.2 %copy-start.2 = (bf16[16,768]{1,0:T(8,128)(2,1)S(1)}, bf16[16,768]{1,0:T(8,128)(2,1)}, u32[]{:S(2)}) copy-start(bf16[16,768]{1,0:T(8,128)(2,1)} %b2_in.1) | copy-start | bytes 73732

commit v5 on v4

--- a/solution.py
+++ b/solution.py
@@ -15,6 +15,7 @@
 
 CROSS_GROUP = 16
 ROW_STEP = 16
+ROW_SHIFT = 4
 SELF_GROUP = 16
 SELF_UNIT = 2
 HEAD_PAD = 16
@@ -30,7 +31,7 @@
 def dense_kernel(pos_sm, len_sm, hid_ref, gain_ref, shift_ref, ab_ref, fb1_ref, fb2_ref,
                  cache_a, cross_a, cache_b, cross_b, aw_hbm, w1_hbm, w2_hbm,
                  hid_out, z_out, cache_a_out, cache_b_out,
-                 w_buf, f1_buf, f2_buf, self_buf, cross_buf, q_s, k_s, v_s, ctx_s, cat_s, lim_s, self_mask, mask_1, mask_2, mask_3, mask_4, order_sm, place_sm,
+                 w_buf, f1_buf, f2_buf, self_buf, cross_buf, q_s, k_s, v_s, ctx_s, cat_s, lim_s, self_mask, mask_1, mask_2, mask_3, mask_4, order_sm, lists_sm,
                  w_sem, f_sem, in_sem, out_sem, cross_sem):
     tok, d_model = hid_ref.shape
     n_heads, self_len, head_dim = self_buf.shape[2:]
@@ -59,32 +60,10 @@
         return pltpu.make_async_copy(self_buf.at[:, rows], cache_out.at[:, rows], out_sem.at[g])
 
     def cross_rows(b):
-        return pl.multiple_of(((len_sm[b] + 15) // 16) * 16, 16)
+        return pl.multiple_of((lax.shift_right_logical(len_sm[b] - 1, ROW_SHIFT) + 1) * ROW_STEP, ROW_STEP)
 
     def length_class(b):
-        return (len_sm[b] + (ROW_STEP - 1)) // ROW_STEP - 1
-
-    def sort_by_length():
-        for k in range(n_class):
-            place_sm[k] = 0
-
-        def count(b, c):
-            k = length_class(b)
-            place_sm[k] = place_sm[k] + 1
-            return c
-        lax.fori_loop(0, tok, count, 0)
-        start = 0
-        for k in range(n_class):
-            here = place_sm[k]
-            place_sm[k] = start
-            start = start + here
-
-        def put(b, c):
-            k = length_class(b)
-            order_sm[place_sm[k]] = b
-            place_sm[k] = place_sm[k] + 1
-            return c
-        lax.fori_loop(0, tok, put, 0)
+        return lax.shift_right_logical(len_sm[b] - 1, ROW_SHIFT)
 
     def cross_copy(cross, b):
         rows = pl.ds(0, cross_rows(b))
@@ -97,24 +76,38 @@
     weight_copy(3).start()
     weight_copy(4).start()
 
-    sort_by_length()
-
-    def first_cross(i, c):
-        cross_copy(cross_a, order_sm[i]).start()
+    def first_cross(b, sizes):
+        cross_copy(cross_a, b).start()
+        k = length_class(b)
+        size = sizes[0]
+        for j in range(1, n_class):
+            size = jnp.where(k == j, sizes[j], size)
+        lists_sm[k * tok + size] = b
+        return tuple(n + jnp.where(k == j, 1, 0) for j, n in enumerate(sizes))
+    sizes = lax.fori_loop(0, tok, first_cross, (jnp.int32(0),) * n_class)
+
+    def place(i, c):
+        at, end = i, jnp.int32(0)
+        for j in range(n_class - 1):
+            end = end + sizes[j]
+            at = jnp.where(i >= end, (j + 1) * tok + i - end, at)
+        order_sm[i] = lists_sm[at]
         return c
-    lax.fori_loop(0, tok, first_cross, 0)
-    weight_copy(5).start()
-    for cp in ffn_copies():
-        cp.start()
-    for i in range(6, 12):
-        weight_copy(i).start()
+    lax.fori_loop(0, tok, place, 0)
 
     def zero_tail(b, c):
         def zero_part(part, c2):
             cross_buf[b, 1, :, pl.ds(pl.multiple_of(part * 16, 16), 16), :] = jnp.zeros((n_heads, 16, head_dim), BF16)
             return c2
-        return lax.fori_loop(cross_rows(b) // 16, src // 16, zero_part, c)
+        return lax.fori_loop(length_class(b) + 1, n_class, zero_part, c)
     lax.fori_loop(0, tok, zero_tail, 0)
+
+    def issue_rest():
+        weight_copy(5).start()
+        for cp in ffn_copies():
+            cp.start()
+        for i in range(6, 12):
+            weight_copy(i).start()
 
     def build_mask(ref, length):
         row = lax.broadcasted_iota(jnp.int32, ref.shape, 0)
@@ -167,6 +160,8 @@
         to_heads(q_s, proj(layer, 0, x))
         to_heads(k_s, proj(layer, 1, x))
         to_heads(v_s, proj(layer, 2, x))
+        if layer == 0:
+            issue_rest()
         row_i = lax.broadcasted_iota(jnp.int32, (self_len, head_dim), 0)
         row_b = row_i.astype(F32).astype(BF16)
 
@@ -279,7 +274,7 @@
             VMEM((2, tok, n_heads, self_len, head_dim), BF16), VMEM((tok, 2, n_heads, src, head_dim), BF16),
             heads, heads, heads, heads, VMEM((tok, d_model), BF16), VMEM((tok * HEAD_PAD, 128), jnp.int32),
             VMEM((2 * HEAD_PAD, 2 * n_heads * self_len), jnp.int32), ] + [VMEM((HEAD_PAD, n_heads * rows), jnp.int32) for rows in range(ROW_STEP, src + 1, ROW_STEP)] + [
-            pltpu.SMEM((tok,), jnp.int32), pltpu.SMEM((8,), jnp.int32),
+            pltpu.SMEM((tok,), jnp.int32), pltpu.SMEM((src // ROW_STEP * tok,), jnp.int32),
             pltpu.SemaphoreType.DMA((12,)), pltpu.SemaphoreType.DMA((2,)), pltpu.SemaphoreType.DMA((n_self,)),
             pltpu.SemaphoreType.DMA((n_self,)), pltpu.SemaphoreType.DMA((tok,)),
         ],
@@ -462,8 +457,8 @@
 
 
 ROWS = 128
-SPLIT = 2
-SLOTS = 6
+SPLIT = 4
+SLOTS = 12
 
 
 def expert_kernel(meta_sm, z_ref, cols_ref, rw_ref, b1_in, b2_in, w1_hbm, w2_hbm, out_ref,

time: 76.9 us -> 76.6 us (level)
  Pallas kernels: 75.6 us -> 74.7 us
    pallas_call x1, Pallas kernels: 13.8 us -> 16.4 us  [reduce_outputs(): pl.pallas_call(reduce_kernel, out_shape=VMEM((tok, d_model), BF16), in_sp...]
    pallas_call x1, Pallas kernels: 34.2 us -> 32.3 us  [dense_layers(): pl.pallas_call(dense_kernel, out_shape=[VMEM((tok, d_model), F32), VMEM((...]
    pallas_call x1, Pallas kernels: 15.6 us -> 13.9 us  [run_experts(): pl.pallas_call(expert_kernel, out_shape=VMEM((group_n, tok, d_model), F32...]
where the time goes in v5:
time: 76.6 us; the launch traced here: 76.1 us
  Pallas kernels  74.7 us (98%)
    pallas_call x1, Pallas kernels, dense_layers(): pl.pallas_call(dense_kernel, out_shape=[VMEM((tok, d_model), F32), VMEM((...  32.3 us
    pallas_call x1, Pallas kernels, reduce_outputs(): pl.pallas_call(reduce_kernel, out_shape=VMEM((tok, d_model), BF16), in_sp...  16.4 us
    pallas_call x1, Pallas kernels, run_experts(): pl.pallas_call(expert_kernel, out_shape=VMEM((group_n, tok, d_model), F32...  13.9 us
    pallas_call x1, Pallas kernels, gather_tokens(): pl.pallas_call(functools.partial(gather_kernel, n_loc), out_shape=[VMEM((...  12.1 us

profile of v5, /device:TPU:0, one launch (start us, length us, event | category | flops | bytes accessed | tf_op | source)
XLA Modules:
  0.0 76.1 jit_solution(2428225514320673006)
XLA Ops:
  0.6 0.0 copy-start.3
  0.6 0.0 copy-start
  0.7 0.0 copy-start.1
  0.7 0.0 copy-start.2
  0.7 32.3 %dense_layers.1 = (f32[64,768]{1,0:T(8,128)S(1)}, bf16[64,768]{1,0:T(8,128)(2,1)S(1)}, bf16[2,64,12,16,64]{4,3,2,1,0:T(8,128)(2,1)}, bf16[2,64,12,16,64]{4,3,2,1,0:T(8,128)(2,1)}) custom-call(s32[64]{0:T(128)} %pos_sm.1, s32[64]{0:T(128)} %len_sm.1, bf16[64,768]{1,0:T(8,128)(2,1)} %hid_ref.1, f32[3,2,768]{2,1,0:T(2,128)} %bitcast.15, f32[3,2,768]{2,1,0:T(2,128)} %bitcast.16, ...), custom_call_target="tpu_custom_call" | custom-call | tf_op jit(solution)/shard_map/dense_layers/pallas_call | solution.py:267
  33.0 0.0 copy-done.3
  33.0 12.1 %gather_tokens.1 = (bf16[8,64,768]{2,1,0:T(8,128)(2,1)S(1)}, f32[512,128]{1,0:T(8,128)S(1)}, s32[8,128]{1,0:T(8,128)S(1)}) custom-call(bf16[64,768]{1,0:T(8,128)(2,1)S(1)} %get-tuple-element.10.z_ref, s32[2,64]{1,0:T(2,128)S(1)} %bitcast.10), custom_call_target="tpu_custom_call" | custom-call | tf_op jit(solution)/shard_map/gather_tokens/pallas_call | solution.py:383
  45.1 0.0 copy-done
  45.1 0.0 copy-done.1
  45.1 0.0 copy-done.2
  45.2 13.9 %run_experts.1.part_ref = f32[8,64,768]{2,1,0:T(8,128)S(1)} custom-call(s32[8,128]{1,0:T(8,128)S(1)} %get-tuple-element.11.meta_sm, bf16[8,64,768]{2,1,0:T(8,128)(2,1)S(1)} %get-tuple-element.12.z_ref, f32[512,128]{1,0:T(8,128)S(1)} %get-tuple-element.13.cols_ref, bf16[768,128]{1,0:T(8,128)(2,1)S(1)} %copy-done, bf16[16,3072]{1,0:T(8,128)(2,1)S(1)} %copy-done.1, ...), custom_call_target="tpu_custom_call" | custom-call | tf_op jit(solution)/shard_map/run_experts/pallas_call | solution.py:565
  59.1 16.4 %reduce_outputs.1 = bf16[64,768]{1,0:T(8,128)(2,1)S(1)} custom-call(f32[8,64,768]{2,1,0:T(8,128)S(1)} %run_experts.1.part_ref, f32[64,768]{1,0:T(8,128)S(1)} %get-tuple-element.14.hid_ref), custom_call_target="tpu_custom_call" | custom-call | tf_op jit(solution)/shard_map/reduce_outputs/pallas_call | solution.py:444
  75.5 0.6 copy.25
Async XLA Ops:
  0.6 32.3 %copy-start.3 = (s32[64,2]{0,1:T(2,128)S(1)}, s32[64,2]{0,1:T(2,128)}, u32[]{:S(2)}) copy-start(s32[64,2]{0,1:T(2,128)} %param.28) | copy-start | bytes 1540
  0.6 44.5 %copy-start = (bf16[768,128]{1,0:T(8,128)(2,1)S(1)}, bf16[768,128]{1,0:T(8,128)(2,1)}, u32[]{:S(2)}) copy-start(bf16[768,128]{1,0:T(8,128)(2,1)} %rw_ref.1) | copy-start | bytes 589828
  0.7 44.5 %copy-start.1 = (bf16[16,3072]{1,0:T(8,128)(2,1)S(1)}, bf16[16,3072]{1,0:T(8,128)(2,1)}, u32[]{:S(2)}) copy-start(bf16[16,3072]{1,0:T(8,128)(2,1)} %b1_in.1) | copy-start | bytes 294916
  0.7 44.5 %copy-start.2 = (bf16[16,768]{1,0:T(8,128)(2,1)S(1)}, bf16[16,768]{1,0:T(8,128)(2,1)}, u32[]{:S(2)}) copy-start(bf16[16,768]{1,0:T(8,128)(2,1)} %b2_in.1) | copy-start | bytes 73732
